TPU v7x, 256 devices: a whole 4x4x8 slice. The times are simulated.
256 devices in a mesh: batch: 2 (over y_lo), space: 64 (over x, y_hi, z), hidden: 2 (over core).
Axes of the slice: x: 4, y: 4 (y_hi: 2, y_lo: 2; y = y_hi * 2 + y_lo), z: 8, core: 2. Of those that a mesh axis runs over, the one named last changes fastest.
Arguments:
- nodes: bfloat16 [2, 8192, 512], P('batch', 'space'), may hold values from -6 to 6
- edges: bfloat16 [2, 65536, 512], P('batch', 'space'), may hold values from -6 to 6
- node_cotangent: bfloat16 [2, 8192, 512], P('batch', 'space'), may hold values from -18 to 18
- edge_cotangent: bfloat16 [2, 65536, 512], P('batch', 'space'), may hold values from -18 to 18
- senders: int32 [65536], P('space'), may hold values from 0 to 255
- receivers: int32 [65536], P('space'), may hold values from 0 to 127
- send_lists: int32 [64, 2, 64], P('space'), may hold values from 0 to 127
- edge_first: bfloat16 [1536, 512], P(None, 'hidden'), may hold values from -0.15625 to 0.15625
- edge_bias: float32 [512], P('hidden'), may hold values from -3 to 3
- edge_second: bfloat16 [512, 512], P('hidden'), may hold values from -0.25 to 0.25
- edge_gain: float32 [512], replicated, may hold values from 0.1 to 1.9
- node_first: bfloat16 [1024, 512], replicated, may hold values from -0.1875 to 0.1875
- node_bias: float32 [512], replicated, may hold values from -3 to 3
- node_second: bfloat16 [512, 512], replicated, may hold values from -0.25 to 0.25
- node_gain: float32 [512], replicated, may hold values from 0.1 to 1.9
Outputs:
- grad_nodes: bfloat16 [2, 8192, 512], P('batch', 'space', 'hidden')
- grad_edges: bfloat16 [2, 65536, 512], P('batch', 'space', 'hidden')
- grad_edge_first: float32 [1536, 512], P(None, 'hidden')
- grad_edge_bias: float32 [512], P('hidden')
- grad_edge_second: float32 [512, 512], P('hidden')
- grad_edge_gain: float32 [512], replicated
- grad_node_first: float32 [1024, 512], replicated
- grad_node_bias: float32 [512], replicated
- grad_node_second: float32 [512, 512], replicated
- grad_node_gain: float32 [512], replicated
Inputs may be any that keep to these rules, and one draw needn't show every extreme that they name: `senders`: an entry below 128 is a local node of the edge's patch; 128 + k is row k of the previous patch's list 1, 192 + k row k of the next patch's list 0. `receivers`: local nodes of the edge's patch. `send_lists`: local nodes of the patch; entries may repeat.
All inputs are finite; a program needn't handle non-finite values.
Results may differ from a plain program's by a relative error of at most 0.015.
Values may be sent and summed in bfloat16 or wider, within the bound.
No kernel may reach another device: no remote copies, remote signals or barrier semaphores. Data moves between devices by JAX's collectives and lax.ppermute only.
A program may use at most 128 MiB of HBM per device.

v0:
```python
import jax
import jax.numpy as jnp
from jax import lax
from jax.experimental import pallas as pl
from jax.experimental.pallas import tpu as pltpu
from jax.sharding import PartitionSpec as P


EPS = 1e-05
BF = jnp.bfloat16
F32 = jnp.float32
ALL = ("batch", "space", "hidden")

NX, NY, NZ = 4, 4, 8
GROUP = 32
PIECE = 224
EXTRA = 8


def device_at(x, y, z, core):
    return ((y % 2) * 64 + (x * 2 + y // 2) * 8 + z) * 2 + core


def place_of(device):
    core, rest = device % 2, device // 2
    b, space = rest // 64, rest % 64
    return space // 16, (space // 8) % 2 * 2 + b, space % 8, core


PLANES = [
    [device_at(x, y, 2 * c + k, core) for x in range(NX) for y in range(NY) for k in range(2)]
    for core in range(2)
    for c in range(NZ // 2)
]


def across_z(bit):
    pairs = []
    for device in range(2 * NX * NY * NZ):
        x, y, z, core = place_of(device)
        pairs.append((device, device_at(x, y, z ^ bit, core)))
    return pairs


def dot(a, b):
    return jnp.dot(a, b, preferred_element_type=F32)


def dot_tn(a, b):
    return lax.dot_general(a, b, (((0,), (0,)), ((), ())), preferred_element_type=F32)


def dot_nt(a, b):
    return lax.dot_general(a, b, (((1,), (1,)), ((), ())), preferred_element_type=F32)


def silu_parts(pre):
    s = 0.5 * jnp.tanh(0.5 * pre) + 0.5
    return pre * s, s * (1.0 + pre * (1.0 - s))


def row_mean(v):
    return jnp.sum(v, axis=1, keepdims=True) * (1.0 / v.shape[1])


def normalize(z):
    centre = z - row_mean(z)
    scale = lax.rsqrt(row_mean(centre * centre) + EPS)
    return centre * scale, scale


def norm_back(g, normed, scale):
    return scale * (g - row_mean(g) - normed * row_mean(g * normed))


def in_hbm(*arrays):
    return tuple(pltpu.with_memory_space_constraint(a, pltpu.HBM) for a in arrays)


def own_columns(width):
    return pl.multiple_of(lax.axis_index("hidden") * width, width)


def copies(pairs, sems, first):
    return [pltpu.make_async_copy(a, b, sems.at[first + i]) for i, (a, b) in enumerate(pairs)]


def pick_kernel(lists, nodes, first, second, lists_v, nodes_v, sems):
    moves = copies([(lists, lists_v), (nodes, nodes_v)], sems, 0)
    for m in moves:
        m.start()
    for m in moves:
        m.wait()
    N, K = nodes_v.shape[0], lists_v.shape[1]
    for i, out in enumerate((first, second)):
        hot = lax.broadcasted_iota(jnp.int32, (N, K), 0) == lists_v[i : i + 1, :]
        out[...] = dot_tn(hot.astype(F32).astype(BF), nodes_v[...]).astype(BF)


def pick(lists, nodes):
    hbm = pl.BlockSpec(memory_space=pltpu.HBM)
    vm = pl.BlockSpec(memory_space=pltpu.VMEM)
    out = jax.ShapeDtypeStruct((lists.shape[1], nodes.shape[1]), BF)
    return pl.pallas_call(
        pick_kernel,
        out_shape=(out, out),
        in_specs=[hbm, hbm],
        out_specs=(vm, vm),
        scratch_shapes=[
            pltpu.VMEM(lists.shape, jnp.int32),
            pltpu.VMEM(nodes.shape, BF),
            pltpu.SemaphoreType.DMA((2,)),
        ],
        compiler_params=pltpu.CompilerParams(vmem_limit_bytes=4 * 1024 * 1024),
        cost_estimate=pl.CostEstimate(flops=200_000_000, bytes_accessed=400_000, transcendentals=0),
        name="pick",
    )(*in_hbm(lists, nodes))


LOADED = 14


def layer_kernel(*refs):
    sources = refs[:LOADED]
    halo_p, halo_n, w1o, b1o, w2o = refs[LOADED : LOADED + 5]
    grads, dh, u, ndx = refs[LOADED + 5 : LOADED + 9]
    loaded = refs[LOADED + 9 : 2 * LOADED + 9]
    (table, tw, hot, act, slope, normed, scale, dz, msum, ndh, ndz, aggr, ginp, sems) = refs[
        2 * LOADED + 9 :
    ]
    snd, rcv, nodes, w1m, b1m, edges, w2m, egain, nf, nb, ns, ngain, ncot, ecot = loaded
    moves = copies(list(zip(sources, loaded)), sems, 0)
    for m in moves:
        m.start()
    E, D = edges.shape
    N = nodes.shape[0]
    H = w1m.shape[1]
    T = table.shape[0]
    half = D // 2
    own = own_columns(half)
    rows = 256
    blocks = E // rows
    side_rows = GROUP * PIECE // 2
    split = (3 * D + 2 * H) // PIECE

    def put(at, value):
        value = value.astype(BF)
        n = value.shape[0]
        done = 0
        while done < n:
            q, off = divmod(at + done, PIECE)
            take = min(n - done, PIECE - off)
            for side in range(2):
                if q < split:
                    piece = q + split * side
                else:
                    piece = 2 * split + (q - split) + (side_rows // PIECE - split) * side
                grads[piece, off : off + take, :] = value[
                    done : done + take, side * 128 : side * 128 + 128
                ]
            done += take

    for m in moves[0:2]:
        m.wait()
    hot[0:T, :] = (lax.broadcasted_iota(jnp.int32, (T, E), 0) == snd[...]).astype(F32).astype(BF)
    hot[T:, :] = (lax.broadcasted_iota(jnp.int32, (N, E), 0) == rcv[...]).astype(F32).astype(BF)
    for m in moves[2:5]:
        m.wait()
    table[0:N, :] = nodes[...]
    table[N : N + halo_p.shape[0], :] = halo_p[...]
    table[N + halo_p.shape[0] :, :] = halo_n[...]
    for side, w in enumerate((w1m, w1o)):
        cols = slice(side * H, side * H + H)
        tw[0:T, cols] = dot(table[...], w[D : 2 * D, :]).astype(BF)
        tw[T:, cols] = dot(nodes[...], w[2 * D :, :]).astype(BF)
    bias = jnp.concatenate([b1m[...], b1o[...]], axis=1)
    aggr[...] = jnp.zeros_like(aggr)
    for m in moves[5:8]:
        m.wait()

    @pl.loop(0, blocks)
    def _(b):
        at = pl.ds(pl.multiple_of(b * rows, rows), rows)
        e = edges[at, :]
        pre = jnp.concatenate([dot(e, w1m[0:D, :]), dot(e, w1o[0:D, :])], axis=1)
        pre = pre + dot_tn(hot[:, at], tw[...]) + bias
        a, sl = silu_parts(pre)
        a = a.astype(BF)
        act[at, :] = a
        slope[at, :] = sl
        z = dot(a[:, 0:H], w2m[...]) + dot(a[:, H:], w2o[...])
        nz, sc = normalize(z)
        normed[at, :] = nz
        scale[at, :] = sc
        message = (egain[...] * nz).astype(BF)
        aggr[...] += dot(hot[T:, at], message)

    for m in moves[8:]:
        m.wait()
    agg = aggr[...].astype(BF)
    ginp[:, 0:D] = nodes[...]
    ginp[:, D:] = agg
    npre = dot(ginp[...], nf[...]) + nb[...]
    nact, nslope = silu_parts(npre)
    nact = nact.astype(BF)
    nnorm, nscale = normalize(dot(nact, ns[...]))
    up = ncot[...].astype(F32)
    gain_n = jnp.sum(up * nnorm, axis=0, keepdims=True)
    dzn = norm_back(ngain[...] * up, nnorm, nscale).astype(BF)
    ndz[...] = dzn
    dhn = (dot_nt(dzn, ns[...]) * nslope).astype(BF)
    ndh[...] = dhn
    bias_n = jnp.sum(dhn.astype(F32), axis=0, keepdims=True)
    put(3 * D + 2 * H, dot_tn(ginp[...], ndh[:, pl.ds(own, half)]))
    put(5 * D + 2 * H, dot_tn(nact, ndz[:, pl.ds(own, half)]))
    dxn = dot_nt(dhn, nf[...])
    ndx[...] = dxn[:, 0:D]
    ag = dxn[:, D:].astype(BF)
    msum[...] = jnp.zeros_like(msum)

    @pl.loop(0, blocks)
    def _(b):
        at = pl.ds(pl.multiple_of(b * rows, rows), rows)
        mg = ecot[at, :].astype(F32) + dot_tn(hot[T:, at], ag)
        nz = normed[at, :]
        msum[0:8, :] += jnp.sum((mg * nz).reshape(rows // 8, 8, D), axis=0)
        d = norm_back(egain[...] * mg, nz, scale[at, :]).astype(BF)
        dz[at, :] = d
        g = jnp.concatenate([dot_nt(d, w2m[...]), dot_nt(d, w2o[...])], axis=1)
        g = (g * slope[at, :]).astype(BF)
        dh[at, :] = g
        msum[8:16, :] += jnp.sum(g.astype(F32).reshape(rows // 8, 8, D), axis=0)

    second = dot_tn(act[:, 0:H], dz[...])
    put(3 * D, second[:, 0:half])
    put(3 * D + H, second[:, half:])
    put(0, dot_tn(edges[...], dh[:, 0:H]))
    u[...] = dot(hot[...], dh[...]).astype(BF)
    put(D, dot_tn(table[...], u[0:T, 0:H]))
    put(2 * D, dot_tn(nodes[...], u[T:, 0:H]))

    gain_e = jnp.sum(msum[0:8, :], axis=0, keepdims=True)
    bias_e = jnp.sum(msum[8:16, :], axis=0, keepdims=True)[:, 0:H]
    parts = []
    for v in (bias_e, gain_e, bias_n, gain_n):
        parts += [v[:, i : i + 128] for i in range(0, v.shape[1], 128)]
    zero = jnp.zeros((2 * EXTRA - len(parts), 128), F32)
    vec = jnp.concatenate(parts + [zero], axis=0).astype(BF)
    for piece in range(GROUP):
        if piece < 2:
            grads[piece, PIECE:, :] = vec[piece * EXTRA : piece * EXTRA + EXTRA]
        else:
            grads[piece, PIECE:, :] = jnp.zeros((EXTRA, 128), BF)


def run_layer(params, arrived):
    N, D = params[2].shape
    H = params[3].shape[1]
    E = params[5].shape[0]
    T = N + 2 * arrived[0].shape[0]
    hbm = pl.BlockSpec(memory_space=pltpu.HBM)
    vm = pl.BlockSpec(memory_space=pltpu.VMEM)
    return pl.pallas_call(
        layer_kernel,
        out_shape=(
            jax.ShapeDtypeStruct((GROUP, PIECE + EXTRA, 128), BF),
            jax.ShapeDtypeStruct((E, 2 * H), BF),
            jax.ShapeDtypeStruct((T + N, 2 * H), BF),
            jax.ShapeDtypeStruct((N, D), F32),
        ),
        in_specs=[hbm] * LOADED + [vm] * len(arrived),
        out_specs=(vm, vm, vm, vm),
        scratch_shapes=[pltpu.VMEM(p.shape, p.dtype) for p in params]
        + [
            pltpu.VMEM((T, D), BF),
            pltpu.VMEM((T + N, 2 * H), BF),
            pltpu.VMEM((T + N, E), BF),
            pltpu.VMEM((E, 2 * H), BF),
            pltpu.VMEM((E, 2 * H), F32),
            pltpu.VMEM((E, D), F32),
            pltpu.VMEM((E, 1), F32),
            pltpu.VMEM((E, D), BF),
            pltpu.VMEM((16, D), F32),
            pltpu.VMEM((N, D), BF),
            pltpu.VMEM((N, D), BF),
            pltpu.VMEM((N, D), F32),
            pltpu.VMEM((N, 2 * D), BF),
            pltpu.SemaphoreType.DMA((LOADED,)),
        ],
        compiler_params=pltpu.CompilerParams(vmem_limit_bytes=40 * 1024 * 1024),
        cost_estimate=pl.CostEstimate(
            flops=6_000_000_000, bytes_accessed=12_000_000, transcendentals=1_000_000
        ),
        name="layer",
    )(*in_hbm(*params), *arrived)


def inputs_kernel(
    w1m, ecot, ncot, w1o, dh, u, ndx, gedges, gnodes, to_prev, to_next, w1m_v, ecot_v, ncot_v, out, sems
):
    D = ncot.shape[1]
    H = w1m.shape[1]
    N = ncot.shape[0]
    T = u.shape[0] - N
    half = D // 2
    own = own_columns(half)
    K = to_prev.shape[0]
    moves = copies(
        [
            (w1m, w1m_v),
            (ecot.at[:, pl.ds(own, half)], ecot_v),
            (ncot.at[:, pl.ds(own, half)], ncot_v),
        ],
        sems,
        0,
    )
    for m in moves:
        m.start()
    moves[0].wait()
    moves[2].wait()
    at_s = pl.ds(pl.multiple_of(D + own, half), half)
    at_r = pl.ds(pl.multiple_of(2 * D + own, half), half)
    tg = dot_nt(u[0:T, 0:H], w1m_v[at_s, :]) + dot_nt(u[0:T, H:], w1o[at_s, :])
    rg = dot_nt(u[T:, 0:H], w1m_v[at_r, :]) + dot_nt(u[T:, H:], w1o[at_r, :])
    to_prev[...] = tg[N : N + K, :].astype(BF)
    to_next[...] = tg[N + K :, :].astype(BF)
    gnodes[...] = ncot_v[...].astype(F32) + ndx[:, pl.ds(own, half)] + tg[0:N] + rg
    moves[1].wait()
    part = dot_nt(dh[:, 0:H], w1m_v[pl.ds(own, half), :]) + dot_nt(
        dh[:, H:], w1o[pl.ds(own, half), :]
    )
    out[...] = (ecot_v[...].astype(F32) + part).astype(BF)
    last = pltpu.make_async_copy(out, gedges, sems.at[3])
    last.start()
    last.wait()


def run_inputs(w1m, ecot, ncot, w1o, dh, u, ndx, halo):
    N, D = ncot.shape
    E = ecot.shape[0]
    half = D // 2
    hbm = pl.BlockSpec(memory_space=pltpu.HBM)
    vm = pl.BlockSpec(memory_space=pltpu.VMEM)
    sent = jax.ShapeDtypeStruct((halo, half), BF)
    return pl.pallas_call(
        inputs_kernel,
        out_shape=(
            jax.ShapeDtypeStruct((E, half), BF),
            jax.ShapeDtypeStruct((N, half), F32),
            sent,
            sent,
        ),
        in_specs=[hbm, hbm, hbm, vm, vm, vm, vm],
        out_specs=(hbm, vm, vm, vm),
        scratch_shapes=[
            pltpu.VMEM(w1m.shape, BF),
            pltpu.VMEM((E, half), BF),
            pltpu.VMEM((N, half), BF),
            pltpu.VMEM((E, half), BF),
            pltpu.SemaphoreType.DMA((4,)),
        ],
        compiler_params=pltpu.CompilerParams(vmem_limit_bytes=12 * 1024 * 1024),
        cost_estimate=pl.CostEstimate(
            flops=700_000_000, bytes_accessed=3_000_000, transcendentals=0
        ),
        name="inputs",
    )(*in_hbm(w1m, ecot, ncot), w1o, dh, u, ndx)


def node_kernel(lists, gnodes, first, second, out, lists_v, sems):
    move = pltpu.make_async_copy(lists, lists_v, sems.at[0])
    move.start()
    move.wait()
    N, K = gnodes.shape[0], first.shape[0]
    total = gnodes[...]
    for i, value in enumerate((first, second)):
        hot = lax.broadcasted_iota(jnp.int32, (N, K), 0) == lists_v[i : i + 1, :]
        total = total + dot(hot.astype(F32).astype(BF), value[...])
    out[...] = total.astype(BF)


def run_node(lists, gnodes, first, second):
    hbm = pl.BlockSpec(memory_space=pltpu.HBM)
    vm = pl.BlockSpec(memory_space=pltpu.VMEM)
    return pl.pallas_call(
        node_kernel,
        out_shape=jax.ShapeDtypeStruct(gnodes.shape, BF),
        in_specs=[hbm, vm, vm, vm],
        out_specs=vm,
        scratch_shapes=[pltpu.VMEM(lists.shape, jnp.int32), pltpu.SemaphoreType.DMA((1,))],
        compiler_params=pltpu.CompilerParams(vmem_limit_bytes=4 * 1024 * 1024),
        cost_estimate=pl.CostEstimate(flops=100_000_000, bytes_accessed=300_000, transcendentals=0),
        name="node_gradient",
    )(*in_hbm(lists), gnodes, first, second)


def edge_out_kernel(full, first, second, v0, v1, v2, v3, first_v, second_v, sems):
    D3, _ = first.shape
    H = second.shape[0]
    half = second.shape[1] // 2
    split = (D3 + 2 * H) // PIECE
    last = GROUP // 2 - split

    def fetch(at, count, put):
        done = 0
        while done < count:
            q, off = divmod(at + done, PIECE)
            take = min(count - done, PIECE - off)
            for side in range(2):
                if q < split:
                    piece = q + split * side
                else:
                    piece = 2 * split + (q - split) + last * side
                put(done, take, side, full[piece, off : off + take, :].astype(F32))
            done += take

    def put_first(done, take, side, value):
        first_v[done : done + take, side * 128 : side * 128 + 128] = value

    fetch(0, D3, put_first)
    moves = copies([(first_v, first), (second_v, second)], sems, 0)
    moves[0].start()
    for part in range(2):

        def put_second(done, take, side, value):
            at = part * half + side * 128
            second_v[done : done + take, at : at + 128] = value

        fetch(D3 + part * H, H, put_second)
    moves[1].start()
    row = 0
    for out in (v0, v1, v2, v3):
        for at in range(0, out.shape[1], 128):
            piece, off = divmod(row, EXTRA)
            tile = full[piece, PIECE:, :].astype(F32)
            out[:, at : at + 128] = tile[off : off + 1, :]
            row += 1
    for m in moves:
        m.wait()


def run_edge_out(full, D, H):
    hbm = pl.BlockSpec(memory_space=pltpu.HBM)
    vm = pl.BlockSpec(memory_space=pltpu.VMEM)
    shapes = [(3 * D, H), (H, D)]
    outs = shapes + [(1, H), (1, D), (1, D), (1, D)]
    return pl.pallas_call(
        edge_out_kernel,
        out_shape=tuple(jax.ShapeDtypeStruct(s, F32) for s in outs),
        in_specs=[vm],
        out_specs=(hbm, hbm, vm, vm, vm, vm),
        scratch_shapes=[pltpu.VMEM(s, F32) for s in shapes] + [pltpu.SemaphoreType.DMA((2,))],
        compiler_params=pltpu.CompilerParams(vmem_limit_bytes=12 * 1024 * 1024),
        cost_estimate=pl.CostEstimate(flops=1_000_000, bytes_accessed=3_000_000, transcendentals=0),
        name="edge_out",
    )(full)


def node_out_kernel(mine, other, first, second, first_v, second_v, sems):
    D2, D = first.shape
    half = D // 2
    mine_at = own_columns(half)
    other_at = pl.multiple_of(half - mine_at, half)
    skip = (3 * D + D2 // 2) % PIECE
    last = mine.shape[0] // 2
    moves = copies([(first_v, first), (second_v, second)], sems, 0)
    for base, count, out, move in ((0, D2, first_v, moves[0]), (D2, D, second_v, moves[1])):
        for src, col in ((mine, mine_at), (other, other_at)):
            done = 0
            while done < count:
                q, off = divmod(skip + base + done, PIECE)
                take = min(count - done, PIECE - off)
                for side in range(2):
                    at = pl.ds(pl.multiple_of(col + side * 128, 128), 128)
                    out[done : done + take, at] = src[q + last * side, off : off + take, :].astype(
                        F32
                    )
                done += take
        move.start()
    for m in moves:
        m.wait()


def run_node_out(mine, other, D):
    hbm = pl.BlockSpec(memory_space=pltpu.HBM)
    vm = pl.BlockSpec(memory_space=pltpu.VMEM)
    shapes = [(2 * D, D), (D, D)]
    return pl.pallas_call(
        node_out_kernel,
        out_shape=tuple(jax.ShapeDtypeStruct(s, F32) for s in shapes),
        in_specs=[vm, vm],
        out_specs=(hbm, hbm),
        scratch_shapes=[pltpu.VMEM(s, F32) for s in shapes] + [pltpu.SemaphoreType.DMA((2,))],
        compiler_params=pltpu.CompilerParams(vmem_limit_bytes=12 * 1024 * 1024),
        cost_estimate=pl.CostEstimate(flops=1_000_000, bytes_accessed=4_000_000, transcendentals=0),
        name="node_out",
    )(mine, other)


def all_pieces(value, groups):
    return lax.all_to_all(value, ALL, 0, 0, axis_index_groups=groups, tiled=True)


def step(
    nodes,
    edges,
    node_cotangent,
    edge_cotangent,
    senders,
    receivers,
    send_lists,
    edge_first,
    edge_bias,
    edge_second,
    edge_gain,
    node_first,
    node_bias,
    node_second,
    node_gain,
):
    swap = [(0, 1), (1, 0)]
    count = lax.axis_size("space")
    onward = [(i, (i + 1) % count) for i in range(count)]
    backward = [((i + 1) % count, i) for i in range(count)]
    rows = nodes[0]
    lists = send_lists[0]
    D = rows.shape[1]
    H = edge_first.shape[1]
    halo = lists.shape[1]

    bias_row = edge_bias[None]
    first_other = lax.ppermute(edge_first, "hidden", swap)
    second_other = lax.ppermute(edge_second, "hidden", swap)
    bias_other = lax.ppermute(bias_row, "hidden", swap)
    list0, list1 = pick(lists, rows)
    from_prev = lax.ppermute(list1, "space", onward)
    from_next = lax.ppermute(list0, "space", backward)

    grads, dh, u, ndx = run_layer(
        (
            senders[None],
            receivers[None],
            rows,
            edge_first,
            bias_row,
            edges[0],
            edge_second,
            edge_gain[None],
            node_first,
            node_bias[None],
            node_second,
            node_gain[None],
            node_cotangent[0],
            edge_cotangent[0],
        ),
        (from_prev, from_next, first_other, bias_other, second_other),
    )
    pieces = all_pieces(grads, PLANES)
    gedges, gnodes, back_prev, back_next = run_inputs(
        edge_first, edge_cotangent[0], node_cotangent[0], first_other, dh, u, ndx, halo
    )
    from_next = lax.ppermute(back_prev, "space", backward)
    from_prev = lax.ppermute(back_next, "space", onward)
    pieces, from_next, from_prev = lax.optimization_barrier((pieces, from_next, from_prev))
    part = jnp.sum(pieces.astype(F32), axis=0).astype(BF)
    for bit in (2, 4):
        near = lax.ppermute(part, ALL, across_z(bit))
        part = (part.astype(F32) + near.astype(F32)).astype(BF)
    full = all_pieces(jnp.broadcast_to(part[None], (GROUP, *part.shape)), PLANES)
    grad_nodes = run_node(lists, gnodes, from_prev, from_next)

    split = (3 * D + 2 * H) // PIECE
    mine = full[2 * split :]
    other = lax.ppermute(mine, "hidden", swap)
    edge_first_grad, edge_second_grad, v0, v1, v2, v3 = run_edge_out(full, D, H)
    node_first_grad, node_second_grad = run_node_out(mine, other, D)
    return (
        grad_nodes[None],
        gedges[None],
        edge_first_grad,
        v0[0],
        edge_second_grad,
        v1[0],
        node_first_grad,
        v2[0],
        node_second_grad,
        v3[0],
    )


def solution(mesh):
    placed = (
        P("batch", "space", None),
        P("batch", "space", None),
        P("batch", "space", None),
        P("batch", "space", None),
        P("space"),
        P("space"),
        P("space", None, None),
        P(None, "hidden"),
        P("hidden"),
        P("hidden", None),
        P(),
        P(),
        P(),
        P(),
        P(),
    )
    return jax.shard_map(
        step,
        mesh=mesh,
        in_specs=placed,
        out_specs=(
            P("batch", "space", "hidden"),
            P("batch", "space", "hidden"),
            P(None, "hidden"),
            P("hidden"),
            P("hidden", None),
            P(),
            P(),
            P(),
            P(),
            P(),
        ),
        check_vma=False,
    )
```

profile of v0, /device:TPU:1, one launch (start us, length us, event | category | flops | bytes accessed | tf_op | source)
XLA Modules:
  0.0 113.9 jit_solution(10482393680401225817)
XLA Ops:
  0.6 3.3 %collective-permute-start = (bf16[1536,256]{1,0:T(8,128)(2,1)}, bf16[1536,256]{1,0:T(8,128)(2,1)S(1)}, u32[]{:S(2)}, u32[]{:S(2)}) collective-permute-start(bf16[1536,256]{1,0:T(8,128)(2,1)} %w1m.1), channel_id=1, source_target_pairs={{0,1},{1,0},{2,3},{3,2},{4,5},{5,4},{6,7},{7,6},{8,9},{9,8},{10,11... | collective-permute-start | bytes 2359304 | tf_op jit(solution)/shard_map/ppermute | solution.py:532
  3.9 0.1 collective-permute-start.4
  4.0 1.2 %pick.1 = (bf16[64,512]{1,0:T(8,128)(2,1)S(1)}, bf16[64,512]{1,0:T(8,128)(2,1)S(1)}) custom-call(s32[2,64]{1,0:T(2,128)} %bitcast.35, bf16[128,512]{1,0:T(8,128)(2,1)} %bitcast.23), custom_call_target="tpu_custom_call" | custom-call | flops 200000000 | bytes 400000 | tf_op jit(solution)/shard_map/pick/pallas_call | solution.py:104
  5.2 0.1 collective-permute-start.1
  5.3 8.8 %collective-permute-start.2 = (bf16[64,512]{1,0:T(8,128)(2,1)S(1)}, bf16[64,512]{1,0:T(8,128)(2,1)S(1)}, u32[]{:S(2)}, u32[]{:S(2)}) collective-permute-start(bf16[64,512]{1,0:T(8,128)(2,1)S(1)} %get-tuple-element.32), channel_id=1, source_target_pairs={{2,0},{4,2},{6,4},{8,6},{10,8},{12,10},{14,12},{16,14},{18,16},{20... | collective-permute-start | bytes 196616 | tf_op jit(solution)/shard_map/ppermute | solution.py:537
  14.1 0.7 collective-permute-start.3
  14.7 1.0 collective-permute-done.3.refs_17_
  15.8 0.3 collective-permute-done.1.refs_14_
  16.0 0.0 collective-permute-done.2.refs_15_
  16.0 0.0 collective-permute-done.4.refs_18_
  16.0 0.0 collective-permute-done.refs_16_.w1o
  16.0 13.5 %layer.1 = (bf16[32,232,128]{2,1,0:T(8,128)(2,1)}, bf16[1024,512]{1,0:T(8,128)(2,1)S(1)}, bf16[384,512]{1,0:T(8,128)(2,1)S(1)}, f32[128,512]{1,0:T(8,128)S(1)}) custom-call(s32[1,1024]{1,0:T(1,128)} %bitcast.25, s32[1,1024]{1,0:T(1,128)} %bitcast.26, bf16[128,512]{1,0:T(8,128)(2,1)} %bitcast.24, bf16[1536,256]{1,0:T(8,128)(2,1)} %w1m.1, f32[1,256]{1,0:T(1,128)} %bitcast.34, ...), custom_call_target="tpu_custom_call" | custom-call | flops 6000000000 | bytes 12000000 | tf_op jit(solution)/shard_map/layer/pallas_call | solution.py:263
  29.5 4.7 %all-to-all-start = ((bf16[32,232,128]{2,1,0:T(8,128)(2,1)}), bf16[32,232,128]{2,1,0:T(8,128)(2,1)}, u32[]{:S(2)}, u32[]{:S(2)}) async-start(bf16[32,232,128]{2,1,0:T(8,128)(2,1)} %get-tuple-element.37), calls=%async_computation | async-start | bytes 3801088 | tf_op jit(solution)/shard_map/all_to_all | solution.py:501
  34.3 3.1 %inputs.1 = (bf16[1024,256]{1,0:T(8,128)(2,1)}, f32[128,256]{1,0:T(8,128)S(1)}, bf16[64,256]{1,0:T(8,128)(2,1)S(1)}, bf16[64,256]{1,0:T(8,128)(2,1)S(1)}) custom-call(bf16[1536,256]{1,0:T(8,128)(2,1)} %w1m.1, bf16[1024,512]{1,0:T(8,128)(2,1)} %bitcast.18, bf16[128,512]{1,0:T(8,128)(2,1)} %bitcast.20, ...), custom_call_target="tpu_custom_call" | custom-call | flops 700000000 | bytes 3000000 | tf_op jit(solution)/shard_map/inputs/pallas_call | solution.py:345
  37.4 9.7 %collective-permute-start.5 = (bf16[64,256]{1,0:T(8,128)(2,1)S(1)}, bf16[64,256]{1,0:T(8,128)(2,1)S(1)}, u32[]{:S(2)}, u32[]{:S(2)}) collective-permute-start(bf16[64,256]{1,0:T(8,128)(2,1)S(1)} %get-tuple-element.38), channel_id=1, source_target_pairs={{2,0},{4,2},{6,4},{8,6},{10,8},{12,10},{14,12},{16,14},{18,16},{20... | collective-permute-start | bytes 98312 | tf_op jit(solution)/shard_map/ppermute | solution.py:562
  47.1 0.0 collective-permute-start.6
  47.1 9.8 %collective-permute-done.5.second = bf16[64,256]{1,0:T(8,128)(2,1)S(1)} collective-permute-done((bf16[64,256]{1,0:T(8,128)(2,1)S(1)}, bf16[64,256]{1,0:T(8,128)(2,1)S(1)}, u32[]{:S(2)}, u32[]{:S(2)}) %collective-permute-start.5) | collective-permute-done | bytes 32800 | tf_op jit(solution)/shard_map/ppermute | solution.py:562
  56.9 0.0 collective-permute-done.6.first
  56.9 5.9 %all-to-all-done = bf16[32,232,128]{2,1,0:T(8,128)(2,1)} async-done(((bf16[32,232,128]{2,1,0:T(8,128)(2,1)}), bf16[32,232,128]{2,1,0:T(8,128)(2,1)}, u32[]{:S(2)}, u32[]{:S(2)}) %all-to-all-start) | async-done | bytes 1900576 | tf_op jit(solution)/shard_map/all_to_all | solution.py:501
  62.9 1.8 %reduce_sum.12 = bf16[232,128]{1,0:T(8,128)(2,1)S(1)} reduce(bf16[32,232,128]{2,1,0:T(8,128)(2,1)} %all-to-all-done, bf16[]{:T(256)} %constant.2.clone.1), dimensions={0}, to_apply=%region_0.0 | reduce | flops 920576 | bytes 1959938 | tf_op jit(solution)/shard_map/reduce_sum | solution.py:565
  64.7 1.6 %collective-permute-start.7 = (bf16[232,128]{1,0:T(8,128)(2,1)S(1)}, bf16[232,128]{1,0:T(8,128)(2,1)S(1)}, u32[]{:S(2)}, u32[]{:S(2)}) collective-permute-start(bf16[232,128]{1,0:T(8,128)(2,1)S(1)} %reduce_sum.12), channel_id=1, source_target_pairs={{0,4},{1,5},{2,6},{3,7},{4,0},{5,1},{6,2},{7,3},{8,12},{9,13},{10,... | collective-permute-start | bytes 178184 | tf_op jit(solution)/shard_map/ppermute | solution.py:567
  66.3 2.4 %collective-permute-done.7 = bf16[232,128]{1,0:T(8,128)(2,1)S(1)} collective-permute-done((bf16[232,128]{1,0:T(8,128)(2,1)S(1)}, bf16[232,128]{1,0:T(8,128)(2,1)S(1)}, u32[]{:S(2)}, u32[]{:S(2)}) %collective-permute-start.7) | collective-permute-done | bytes 59424 | tf_op jit(solution)/shard_map/ppermute | solution.py:567
  68.7 5.0 %collective-permute-start.8 = (bf16[232,128]{1,0:T(8,128)(2,1)S(1)}, bf16[232,128]{1,0:T(8,128)(2,1)S(1)}, u32[]{:S(2)}, u32[]{:S(2)}) collective-permute-start(bf16[232,128]{1,0:T(8,128)(2,1)S(1)} %add_convert_fusion.1), channel_id=1, source_target_pairs={{0,8},{1,9},{2,10},{3,11},{4,12},{5,13},{6,14},{7,15},{8,0},{9,1},... | collective-permute-start | bytes 178184 | tf_op jit(solution)/shard_map/ppermute | solution.py:567
  73.7 2.2 %collective-permute-done.8 = bf16[232,128]{1,0:T(8,128)(2,1)S(1)} collective-permute-done((bf16[232,128]{1,0:T(8,128)(2,1)S(1)}, bf16[232,128]{1,0:T(8,128)(2,1)S(1)}, u32[]{:S(2)}, u32[]{:S(2)}) %collective-permute-start.8) | collective-permute-done | bytes 59424 | tf_op jit(solution)/shard_map/ppermute | solution.py:567
  75.9 0.2 broadcast_in_dim.38
  76.1 26.7 %all_to_all.10.full = bf16[32,232,128]{2,1,0:T(8,128)(2,1)S(1)} all-to-all(bf16[32,232,128]{2,1,0:T(8,128)(2,1)S(1)} %broadcast_in_dim.38), channel_id=1, replica_groups={{0,2,128,130,16,18,144,146,32,34,160,162,48,50,176,178,64,66,192,194,80..., dimensions={0} | all-to-all | bytes 3801088 | tf_op jit(solution)/shard_map/all_to_all | solution.py:501
  102.9 0.1 slice.4.mine
  102.9 5.5 %collective-permute-start.9 = (bf16[14,232,128]{2,1,0:T(8,128)(2,1)S(1)}, bf16[14,232,128]{2,1,0:T(8,128)(2,1)S(1)}, u32[]{:S(2)}, u32[]{:S(2)}) collective-permute-start(bf16[14,232,128]{2,1,0:T(8,128)(2,1)S(1)} %slice.4.mine), channel_id=1, source_target_pairs={{0,1},{1,0},{2,3},{3,2},{4,5},{5,4},{6,7},{7,6},{8,9},{9,8},{10,11... | collective-permute-start | bytes 2494472 | tf_op jit(solution)/shard_map/ppermute | solution.py:574
  108.4 1.5 %node_gradient.1 = bf16[128,256]{1,0:T(8,128)(2,1)} custom-call(s32[2,64]{1,0:T(2,128)} %bitcast.36, f32[128,256]{1,0:T(8,128)S(1)} %get-tuple-element.36.gnodes, bf16[64,256]{1,0:T(8,128)(2,1)S(1)} %collective-permute-done.6.first, bf16[64,256]{1,0:T(8,128)(2,1)S(1)} %collective-permute-done.5.second), custom_call_target="tpu_custom_call" | custom-call | flops 100000000 | bytes 300000 | tf_op jit(solution)/shard_map/node_gradient/pallas_call | solution.py:385
  109.9 2.0 %edge_out.1 = (f32[1536,256]{1,0:T(8,128)}, f32[256,512]{1,0:T(8,128)}, f32[1,256]{1,0:T(1,128)}, f32[1,512]{1,0:T(1,128)}, f32[1,512]{1,0:T(1,128)}, /*index=5*/f32[1,512]{1,0:T(1,128)}) custom-call(bf16[32,232,128]{2,1,0:T(8,128)(2,1)S(1)} %all_to_all.10.full), custom_call_target="tpu_custom_call" | custom-call | flops 1000000 | bytes 3000000 | tf_op jit(solution)/shard_map/edge_out/pallas_call | solution.py:447
  111.9 0.0 collective-permute-done.9.other
  111.9 2.0 %node_out.1 = (f32[1024,512]{1,0:T(8,128)}, f32[512,512]{1,0:T(8,128)}) custom-call(bf16[14,232,128]{2,1,0:T(8,128)(2,1)S(1)} %slice.4.mine, bf16[14,232,128]{2,1,0:T(8,128)(2,1)S(1)} %collective-permute-done.9.other), custom_call_target="tpu_custom_call" | custom-call | flops 1000000 | bytes 4000000 | tf_op jit(solution)/shard_map/node_out/pallas_call | solution.py:488
  (2 shorter events, 0.0 us)
Async XLA Ops:
  0.6 15.4 %collective-permute-start = (bf16[1536,256]{1,0:T(8,128)(2,1)}, bf16[1536,256]{1,0:T(8,128)(2,1)S(1)}, u32[]{:S(2)}, u32[]{:S(2)}) collective-permute-start(bf16[1536,256]{1,0:T(8,128)(2,1)} %w1m.1), channel_id=1, source_target_pairs={{0,1},{1,0},{2,3},{3,2},{4,5},{5,4},{6,7},{7,6},{8,9},{9,8},{10,11... | collective-permute-start | bytes 2359304 | tf_op jit(solution)/shard_map/ppermute | solution.py:532
  3.9 12.1 %collective-permute-start.4 = (bf16[256,512]{1,0:T(8,128)(2,1)}, bf16[256,512]{1,0:T(8,128)(2,1)S(1)}, u32[]{:S(2)}, u32[]{:S(2)}) collective-permute-start(bf16[256,512]{1,0:T(8,128)(2,1)} %refs_6_.1), channel_id=1, source_target_pairs={{0,1},{1,0},{2,3},{3,2},{4,5},{5,4},{6,7},{7,6},{8,9},{9,8},{10,11... | collective-permute-start | bytes 786440 | tf_op jit(solution)/shard_map/ppermute | solution.py:533
  5.2 10.8 %collective-permute-start.1 = (bf16[64,512]{1,0:T(8,128)(2,1)S(1)}, bf16[64,512]{1,0:T(8,128)(2,1)S(1)}, u32[]{:S(2)}, u32[]{:S(2)}) collective-permute-start(bf16[64,512]{1,0:T(8,128)(2,1)S(1)} %get-tuple-element.31), channel_id=1, source_target_pairs={{0,2},{2,4},{4,6},{6,8},{8,10},{10,12},{12,14},{14,16},{16,18},{18... | collective-permute-start | bytes 196616 | tf_op jit(solution)/shard_map/ppermute | solution.py:536
  5.3 10.7 %collective-permute-start.2 = (bf16[64,512]{1,0:T(8,128)(2,1)S(1)}, bf16[64,512]{1,0:T(8,128)(2,1)S(1)}, u32[]{:S(2)}, u32[]{:S(2)}) collective-permute-start(bf16[64,512]{1,0:T(8,128)(2,1)S(1)} %get-tuple-element.32), channel_id=1, source_target_pairs={{2,0},{4,2},{6,4},{8,6},{10,8},{12,10},{14,12},{16,14},{18,16},{20... | collective-permute-start | bytes 196616 | tf_op jit(solution)/shard_map/ppermute | solution.py:537
  14.1 1.7 %collective-permute-start.3 = (f32[1,256]{1,0:T(1,128)}, f32[1,256]{1,0:T(1,128)S(1)}, u32[]{:S(2)}, u32[]{:S(2)}) collective-permute-start(f32[1,256]{1,0:T(1,128)} %bitcast.33), channel_id=1, source_target_pairs={{0,1},{1,0},{2,3},{3,2},{4,5},{5,4},{6,7},{7,6},{8,9},{9,8},{10,11... | collective-permute-start | bytes 3080 | tf_op jit(solution)/shard_map/ppermute | solution.py:534
  29.5 33.3 %all-to-all-start = ((bf16[32,232,128]{2,1,0:T(8,128)(2,1)}), bf16[32,232,128]{2,1,0:T(8,128)(2,1)}, u32[]{:S(2)}, u32[]{:S(2)}) async-start(bf16[32,232,128]{2,1,0:T(8,128)(2,1)} %get-tuple-element.37), calls=%async_computation | async-start | bytes 3801088 | tf_op jit(solution)/shard_map/all_to_all | solution.py:501
  37.4 19.6 %collective-permute-start.5 = (bf16[64,256]{1,0:T(8,128)(2,1)S(1)}, bf16[64,256]{1,0:T(8,128)(2,1)S(1)}, u32[]{:S(2)}, u32[]{:S(2)}) collective-permute-start(bf16[64,256]{1,0:T(8,128)(2,1)S(1)} %get-tuple-element.38), channel_id=1, source_target_pairs={{2,0},{4,2},{6,4},{8,6},{10,8},{12,10},{14,12},{16,14},{18,16},{20... | collective-permute-start | bytes 98312 | tf_op jit(solution)/shard_map/ppermute | solution.py:562
  47.1 9.8 %collective-permute-start.6 = (bf16[64,256]{1,0:T(8,128)(2,1)S(1)}, bf16[64,256]{1,0:T(8,128)(2,1)S(1)}, u32[]{:S(2)}, u32[]{:S(2)}) collective-permute-start(bf16[64,256]{1,0:T(8,128)(2,1)S(1)} %get-tuple-element.39), channel_id=1, source_target_pairs={{0,2},{2,4},{4,6},{6,8},{8,10},{10,12},{12,14},{14,16},{16,18},{18... | collective-permute-start | bytes 98312 | tf_op jit(solution)/shard_map/ppermute | solution.py:563
  64.7 4.0 %collective-permute-start.7 = (bf16[232,128]{1,0:T(8,128)(2,1)S(1)}, bf16[232,128]{1,0:T(8,128)(2,1)S(1)}, u32[]{:S(2)}, u32[]{:S(2)}) collective-permute-start(bf16[232,128]{1,0:T(8,128)(2,1)S(1)} %reduce_sum.12), channel_id=1, source_target_pairs={{0,4},{1,5},{2,6},{3,7},{4,0},{5,1},{6,2},{7,3},{8,12},{9,13},{10,... | collective-permute-start | bytes 178184 | tf_op jit(solution)/shard_map/ppermute | solution.py:567
  68.7 7.1 %collective-permute-start.8 = (bf16[232,128]{1,0:T(8,128)(2,1)S(1)}, bf16[232,128]{1,0:T(8,128)(2,1)S(1)}, u32[]{:S(2)}, u32[]{:S(2)}) collective-permute-start(bf16[232,128]{1,0:T(8,128)(2,1)S(1)} %add_convert_fusion.1), channel_id=1, source_target_pairs={{0,8},{1,9},{2,10},{3,11},{4,12},{5,13},{6,14},{7,15},{8,0},{9,1},... | collective-permute-start | bytes 178184 | tf_op jit(solution)/shard_map/ppermute | solution.py:567
  102.9 9.0 %collective-permute-start.9 = (bf16[14,232,128]{2,1,0:T(8,128)(2,1)S(1)}, bf16[14,232,128]{2,1,0:T(8,128)(2,1)S(1)}, u32[]{:S(2)}, u32[]{:S(2)}) collective-permute-start(bf16[14,232,128]{2,1,0:T(8,128)(2,1)S(1)} %slice.4.mine), channel_id=1, source_target_pairs={{0,1},{1,0},{2,3},{3,2},{4,5},{5,4},{6,7},{7,6},{8,9},{9,8},{10,11... | collective-permute-start | bytes 2494472 | tf_op jit(solution)/shard_map/ppermute | solution.py:574
where the time goes:
time: 114 us
  starting transfers between devices  39.5 us (35%)
  blocking collectives  26.7 us (23%)
  Pallas kernels  23.2 us (20%)
  waiting for transfers between devices  21.6 us (19%)
  other arithmetic  1.83 us (2%)
    all_to_all x1, blocking collectives, all_pieces(): lax.all_to_all(value, ALL, 0, 0, axis_index_groups=groups, tiled=True)  26.7 us
    pallas_call x1, Pallas kernels, run_layer(): pl.pallas_call(layer_kernel, out_shape=(jax.ShapeDtypeStruct((GROUP, PIEC...  13.5 us
    ppermute x1, waiting for transfers between devices, step(): from_next = lax.ppermute(back_prev, 'space', backward)  9.83 us
    ppermute x1, starting transfers between devices, step(): from_next = lax.ppermute(back_prev, 'space', backward)  9.72 us
    ppermute x1, starting transfers between devices, step(): from_next = lax.ppermute(list0, 'space', backward)  8.77 us
    ppermute x2, starting transfers between devices, step(): near = lax.ppermute(part, ALL, across_z(bit))  6.63 us
    all_to_all x1, waiting for transfers between devices, all_pieces(): lax.all_to_all(value, ALL, 0, 0, axis_index_groups=groups, tiled=True)  5.93 us
    ppermute x1, starting transfers between devices, step(): other = lax.ppermute(mine, 'hidden', swap)  5.47 us
  transfers between devices with their start and end apart: 11, of which 6 were waited for; matrix products, arithmetic and copies ran while one was open for 0% of the time, Pallas kernels for 7%

commit v1 on v0

--- a/solution.py
+++ b/solution.py
@@ -34,11 +34,12 @@
 ]
 
 
-def across_z(bit):
+def across_z(first):
     pairs = []
     for device in range(2 * NX * NY * NZ):
         x, y, z, core = place_of(device)
-        pairs.append((device, device_at(x, y, z ^ bit, core)))
+        up = (z // 2) % 2 == (0 if first else 1)
+        pairs.append((device, device_at(x, y, (z + (2 if up else NZ - 2)) % NZ, core)))
     return pairs
 
 
@@ -120,26 +121,84 @@
 LOADED = 14
 
 
-def layer_kernel(*refs):
+def early_kernel(*refs):
     sources = refs[:LOADED]
-    halo_p, halo_n, w1o, b1o, w2o = refs[LOADED : LOADED + 5]
-    grads, dh, u, ndx = refs[LOADED + 5 : LOADED + 9]
-    loaded = refs[LOADED + 9 : 2 * LOADED + 9]
-    (table, tw, hot, act, slope, normed, scale, dz, msum, ndh, ndz, aggr, ginp, sems) = refs[
-        2 * LOADED + 9 :
-    ]
-    snd, rcv, nodes, w1m, b1m, edges, w2m, egain, nf, nb, ns, ngain, ncot, ecot = loaded
-    moves = copies(list(zip(sources, loaded)), sems, 0)
+    loaded = refs[LOADED : 2 * LOADED - 2]
+    hot, part, snd, rcv, sems = refs[2 * LOADED - 2 :]
+    moves = copies(list(zip(sources, (snd, rcv) + tuple(loaded))), sems, 0)
     for m in moves:
         m.start()
+    nodes, w1m = loaded[0], loaded[1]
+    D = nodes.shape[1]
+    N, E = nodes.shape[0], snd.shape[1]
+    T = hot.shape[0] - N
+    for m in moves[0:2]:
+        m.wait()
+    hot[0:T, :] = (lax.broadcasted_iota(jnp.int32, (T, E), 0) == snd[...]).astype(F32).astype(BF)
+    hot[T:, :] = (lax.broadcasted_iota(jnp.int32, (N, E), 0) == rcv[...]).astype(F32).astype(BF)
+    for m in moves[2:4]:
+        m.wait()
+    part[0:N, :] = dot(nodes[...], w1m[D : 2 * D, :]).astype(BF)
+    part[N:, :] = dot(nodes[...], w1m[2 * D :, :]).astype(BF)
+    for m in moves[4:]:
+        m.wait()
+
+
+def run_early(params, halo):
+    N = params[2].shape[0]
+    E = params[5].shape[0]
+    H = params[3].shape[1]
+    hbm = pl.BlockSpec(memory_space=pltpu.HBM)
+    vm = pl.BlockSpec(memory_space=pltpu.VMEM)
+    outs = [pltpu.VMEM(p.shape, p.dtype) for p in params[2:]]
+    outs += [pltpu.VMEM((2 * N + 2 * halo, E), BF), pltpu.VMEM((2 * N, H), BF)]
+    return pl.pallas_call(
+        early_kernel,
+        out_shape=tuple(outs),
+        in_specs=[hbm] * LOADED,
+        out_specs=(vm,) * len(outs),
+        scratch_shapes=[
+            pltpu.VMEM(params[0].shape, jnp.int32),
+            pltpu.VMEM(params[1].shape, jnp.int32),
+            pltpu.SemaphoreType.DMA((LOADED,)),
+        ],
+        compiler_params=pltpu.CompilerParams(vmem_limit_bytes=8 * 1024 * 1024),
+        cost_estimate=pl.CostEstimate(
+            flops=1_500_000_000, bytes_accessed=8_000_000, transcendentals=0
+        ),
+        name="early",
+    )(*in_hbm(*params))
+
+
+def layer_kernel(*refs):
+    loaded = refs[:LOADED]
+    halo_p, halo_n, w1o, b1o, w2o = refs[LOADED : LOADED + 5]
+    grads, gedges, gnodes, to_prev, to_next = refs[LOADED + 5 : LOADED + 10]
+    (
+        table,
+        tw,
+        act,
+        slope,
+        normed,
+        scale,
+        dz,
+        dh,
+        msum,
+        ndh,
+        ndz,
+        ndx,
+        aggr,
+        ginp,
+        ge,
+        sems,
+    ) = refs[LOADED + 10 :]
+    nodes, w1m, b1m, edges, w2m, egain, nf, nb, ns, ngain, ncot, ecot, hot, early = loaded
     E, D = edges.shape
     N = nodes.shape[0]
     H = w1m.shape[1]
     T = table.shape[0]
     half = D // 2
     own = own_columns(half)
-    rows = 256
-    blocks = E // rows
     side_rows = GROUP * PIECE // 2
     split = (3 * D + 2 * H) // PIECE
 
@@ -160,43 +219,31 @@
                 ]
             done += take
 
-    for m in moves[0:2]:
-        m.wait()
-    hot[0:T, :] = (lax.broadcasted_iota(jnp.int32, (T, E), 0) == snd[...]).astype(F32).astype(BF)
-    hot[T:, :] = (lax.broadcasted_iota(jnp.int32, (N, E), 0) == rcv[...]).astype(F32).astype(BF)
-    for m in moves[2:5]:
-        m.wait()
     table[0:N, :] = nodes[...]
     table[N : N + halo_p.shape[0], :] = halo_p[...]
     table[N + halo_p.shape[0] :, :] = halo_n[...]
-    for side, w in enumerate((w1m, w1o)):
-        cols = slice(side * H, side * H + H)
-        tw[0:T, cols] = dot(table[...], w[D : 2 * D, :]).astype(BF)
-        tw[T:, cols] = dot(nodes[...], w[2 * D :, :]).astype(BF)
+    tw[0:N, 0:H] = early[0:N, :]
+    tw[T:, 0:H] = early[N:, :]
+    tw[N:T, 0:H] = dot(table[N:, :], w1m[D : 2 * D, :]).astype(BF)
+    tw[0:T, H:] = dot(table[...], w1o[D : 2 * D, :]).astype(BF)
+    tw[T:, H:] = dot(nodes[...], w1o[2 * D :, :]).astype(BF)
     bias = jnp.concatenate([b1m[...], b1o[...]], axis=1)
     aggr[...] = jnp.zeros_like(aggr)
-    for m in moves[5:8]:
-        m.wait()
-
-    @pl.loop(0, blocks)
-    def _(b):
-        at = pl.ds(pl.multiple_of(b * rows, rows), rows)
-        e = edges[at, :]
-        pre = jnp.concatenate([dot(e, w1m[0:D, :]), dot(e, w1o[0:D, :])], axis=1)
-        pre = pre + dot_tn(hot[:, at], tw[...]) + bias
-        a, sl = silu_parts(pre)
-        a = a.astype(BF)
-        act[at, :] = a
-        slope[at, :] = sl
-        z = dot(a[:, 0:H], w2m[...]) + dot(a[:, H:], w2o[...])
-        nz, sc = normalize(z)
-        normed[at, :] = nz
-        scale[at, :] = sc
-        message = (egain[...] * nz).astype(BF)
-        aggr[...] += dot(hot[T:, at], message)
-
-    for m in moves[8:]:
-        m.wait()
+
+    e = edges[...]
+    pre = jnp.concatenate([dot(e, w1m[0:D, :]), dot(e, w1o[0:D, :])], axis=1)
+    pre = pre + dot_tn(hot[...], tw[...]) + bias
+    a, sl = silu_parts(pre)
+    a = a.astype(BF)
+    act[...] = a
+    slope[...] = sl
+    z = dot(a[:, 0:H], w2m[...]) + dot(a[:, H:], w2o[...])
+    nz, sc = normalize(z)
+    normed[...] = nz
+    scale[...] = sc
+    message = (egain[...] * nz).astype(BF)
+    aggr[...] += dot(hot[T:, :], message)
+
     agg = aggr[...].astype(BF)
     ginp[:, 0:D] = nodes[...]
     ginp[:, D:] = agg
@@ -218,24 +265,35 @@
     ag = dxn[:, D:].astype(BF)
     msum[...] = jnp.zeros_like(msum)
 
-    @pl.loop(0, blocks)
-    def _(b):
-        at = pl.ds(pl.multiple_of(b * rows, rows), rows)
-        mg = ecot[at, :].astype(F32) + dot_tn(hot[T:, at], ag)
-        nz = normed[at, :]
-        msum[0:8, :] += jnp.sum((mg * nz).reshape(rows // 8, 8, D), axis=0)
-        d = norm_back(egain[...] * mg, nz, scale[at, :]).astype(BF)
-        dz[at, :] = d
-        g = jnp.concatenate([dot_nt(d, w2m[...]), dot_nt(d, w2o[...])], axis=1)
-        g = (g * slope[at, :]).astype(BF)
-        dh[at, :] = g
-        msum[8:16, :] += jnp.sum(g.astype(F32).reshape(rows // 8, 8, D), axis=0)
-
+    mg = ecot[...].astype(F32) + dot_tn(hot[T:, :], ag)
+    nz = normed[...]
+    msum[0:8, :] += jnp.sum((mg * nz).reshape(E // 8, 8, D), axis=0)
+    d = norm_back(egain[...] * mg, nz, scale[...]).astype(BF)
+    dz[...] = d
+    g = jnp.concatenate([dot_nt(d, w2m[...]), dot_nt(d, w2o[...])], axis=1)
+    g = (g * slope[...]).astype(BF)
+    dh[...] = g
+    msum[8:16, :] += jnp.sum(g.astype(F32).reshape(E // 8, 8, D), axis=0)
+    part = dot_nt(g[:, 0:H], w1m[pl.ds(own, half), :]) + dot_nt(
+        g[:, H:], w1o[pl.ds(own, half), :]
+    )
+    ge[...] = (ecot[:, pl.ds(own, half)].astype(F32) + part).astype(BF)
+
+    last = pltpu.make_async_copy(ge, gedges, sems.at[0])
+    last.start()
+    u = dot(hot[...], dh[...]).astype(BF)
+    K = halo_p.shape[0]
+    at_s = pl.ds(pl.multiple_of(D + own, half), half)
+    at_r = pl.ds(pl.multiple_of(2 * D + own, half), half)
+    tg = dot_nt(u[0:T, 0:H], w1m[at_s, :]) + dot_nt(u[0:T, H:], w1o[at_s, :])
+    rg = dot_nt(u[T:, 0:H], w1m[at_r, :]) + dot_nt(u[T:, H:], w1o[at_r, :])
+    to_prev[...] = tg[N : N + K, :].astype(BF)
+    to_next[...] = tg[N + K :, :].astype(BF)
+    gnodes[...] = ncot[:, pl.ds(own, half)].astype(F32) + ndx[:, pl.ds(own, half)] + tg[0:N] + rg
     second = dot_tn(act[:, 0:H], dz[...])
     put(3 * D, second[:, 0:half])
     put(3 * D + H, second[:, half:])
     put(0, dot_tn(edges[...], dh[:, 0:H]))
-    u[...] = dot(hot[...], dh[...]).astype(BF)
     put(D, dot_tn(table[...], u[0:T, 0:H]))
     put(2 * D, dot_tn(nodes[...], u[T:, 0:H]))
 
@@ -251,12 +309,16 @@
             grads[piece, PIECE:, :] = vec[piece * EXTRA : piece * EXTRA + EXTRA]
         else:
             grads[piece, PIECE:, :] = jnp.zeros((EXTRA, 128), BF)
+    last.wait()
+
+
+LAYER_VMEM = 26 * 1024 * 1024
 
 
 def run_layer(params, arrived):
-    N, D = params[2].shape
-    H = params[3].shape[1]
-    E = params[5].shape[0]
+    N, D = params[0].shape
+    H = params[1].shape[1]
+    E = params[3].shape[0]
     T = N + 2 * arrived[0].shape[0]
     hbm = pl.BlockSpec(memory_space=pltpu.HBM)
     vm = pl.BlockSpec(memory_space=pltpu.VMEM)
@@ -264,107 +326,37 @@
         layer_kernel,
         out_shape=(
             jax.ShapeDtypeStruct((GROUP, PIECE + EXTRA, 128), BF),
-            jax.ShapeDtypeStruct((E, 2 * H), BF),
-            jax.ShapeDtypeStruct((T + N, 2 * H), BF),
-            jax.ShapeDtypeStruct((N, D), F32),
+            jax.ShapeDtypeStruct((E, D // 2), BF),
+            jax.ShapeDtypeStruct((N, D // 2), F32),
+            jax.ShapeDtypeStruct((arrived[0].shape[0], D // 2), BF),
+            jax.ShapeDtypeStruct((arrived[0].shape[0], D // 2), BF),
         ),
-        in_specs=[hbm] * LOADED + [vm] * len(arrived),
-        out_specs=(vm, vm, vm, vm),
-        scratch_shapes=[pltpu.VMEM(p.shape, p.dtype) for p in params]
-        + [
+        in_specs=[vm] * (LOADED + len(arrived)),
+        out_specs=(vm, hbm, vm, vm, vm),
+        scratch_shapes=[
             pltpu.VMEM((T, D), BF),
             pltpu.VMEM((T + N, 2 * H), BF),
-            pltpu.VMEM((T + N, E), BF),
             pltpu.VMEM((E, 2 * H), BF),
             pltpu.VMEM((E, 2 * H), F32),
             pltpu.VMEM((E, D), F32),
             pltpu.VMEM((E, 1), F32),
             pltpu.VMEM((E, D), BF),
+            pltpu.VMEM((E, 2 * H), BF),
             pltpu.VMEM((16, D), F32),
             pltpu.VMEM((N, D), BF),
             pltpu.VMEM((N, D), BF),
             pltpu.VMEM((N, D), F32),
+            pltpu.VMEM((N, D), F32),
             pltpu.VMEM((N, 2 * D), BF),
-            pltpu.SemaphoreType.DMA((LOADED,)),
+            pltpu.VMEM((E, D // 2), BF),
+            pltpu.SemaphoreType.DMA((1,)),
         ],
-        compiler_params=pltpu.CompilerParams(vmem_limit_bytes=40 * 1024 * 1024),
+        compiler_params=pltpu.CompilerParams(vmem_limit_bytes=LAYER_VMEM),
         cost_estimate=pl.CostEstimate(
             flops=6_000_000_000, bytes_accessed=12_000_000, transcendentals=1_000_000
         ),
         name="layer",
-    )(*in_hbm(*params), *arrived)
-
-
-def inputs_kernel(
-    w1m, ecot, ncot, w1o, dh, u, ndx, gedges, gnodes, to_prev, to_next, w1m_v, ecot_v, ncot_v, out, sems
-):
-    D = ncot.shape[1]
-    H = w1m.shape[1]
-    N = ncot.shape[0]
-    T = u.shape[0] - N
-    half = D // 2
-    own = own_columns(half)
-    K = to_prev.shape[0]
-    moves = copies(
-        [
-            (w1m, w1m_v),
-            (ecot.at[:, pl.ds(own, half)], ecot_v),
-            (ncot.at[:, pl.ds(own, half)], ncot_v),
-        ],
-        sems,
-        0,
-    )
-    for m in moves:
-        m.start()
-    moves[0].wait()
-    moves[2].wait()
-    at_s = pl.ds(pl.multiple_of(D + own, half), half)
-    at_r = pl.ds(pl.multiple_of(2 * D + own, half), half)
-    tg = dot_nt(u[0:T, 0:H], w1m_v[at_s, :]) + dot_nt(u[0:T, H:], w1o[at_s, :])
-    rg = dot_nt(u[T:, 0:H], w1m_v[at_r, :]) + dot_nt(u[T:, H:], w1o[at_r, :])
-    to_prev[...] = tg[N : N + K, :].astype(BF)
-    to_next[...] = tg[N + K :, :].astype(BF)
-    gnodes[...] = ncot_v[...].astype(F32) + ndx[:, pl.ds(own, half)] + tg[0:N] + rg
-    moves[1].wait()
-    part = dot_nt(dh[:, 0:H], w1m_v[pl.ds(own, half), :]) + dot_nt(
-        dh[:, H:], w1o[pl.ds(own, half), :]
-    )
-    out[...] = (ecot_v[...].astype(F32) + part).astype(BF)
-    last = pltpu.make_async_copy(out, gedges, sems.at[3])
-    last.start()
-    last.wait()
-
-
-def run_inputs(w1m, ecot, ncot, w1o, dh, u, ndx, halo):
-    N, D = ncot.shape
-    E = ecot.shape[0]
-    half = D // 2
-    hbm = pl.BlockSpec(memory_space=pltpu.HBM)
-    vm = pl.BlockSpec(memory_space=pltpu.VMEM)
-    sent = jax.ShapeDtypeStruct((halo, half), BF)
-    return pl.pallas_call(
-        inputs_kernel,
-        out_shape=(
-            jax.ShapeDtypeStruct((E, half), BF),
-            jax.ShapeDtypeStruct((N, half), F32),
-            sent,
-            sent,
-        ),
-        in_specs=[hbm, hbm, hbm, vm, vm, vm, vm],
-        out_specs=(hbm, vm, vm, vm),
-        scratch_shapes=[
-            pltpu.VMEM(w1m.shape, BF),
-            pltpu.VMEM((E, half), BF),
-            pltpu.VMEM((N, half), BF),
-            pltpu.VMEM((E, half), BF),
-            pltpu.SemaphoreType.DMA((4,)),
-        ],
-        compiler_params=pltpu.CompilerParams(vmem_limit_bytes=12 * 1024 * 1024),
-        cost_estimate=pl.CostEstimate(
-            flops=700_000_000, bytes_accessed=3_000_000, transcendentals=0
-        ),
-        name="inputs",
-    )(*in_hbm(w1m, ecot, ncot), w1o, dh, u, ndx)
+    )(*params, *arrived)
 
 
 def node_kernel(lists, gnodes, first, second, out, lists_v, sems):
@@ -394,7 +386,9 @@
     )(*in_hbm(lists), gnodes, first, second)
 
 
-def edge_out_kernel(full, first, second, v0, v1, v2, v3, first_v, second_v, sems):
+def edge_out_kernel(
+    full, first, second, v0, v1, v2, v3, nfirst, nsecond, first_v, second_v, nfirst_v, nsecond_v, sems
+):
     D3, _ = first.shape
     H = second.shape[0]
     half = second.shape[1] // 2
@@ -418,7 +412,18 @@
         first_v[done : done + take, side * 128 : side * 128 + 128] = value
 
     fetch(0, D3, put_first)
-    moves = copies([(first_v, first), (second_v, second)], sems, 0)
+    D2, D = nfirst.shape
+    cols = pl.ds(own_columns(D // 2), D // 2)
+    moves = copies(
+        [
+            (first_v, first),
+            (second_v, second),
+            (nfirst_v, nfirst.at[:, cols]),
+            (nsecond_v, nsecond.at[:, cols]),
+        ],
+        sems,
+        0,
+    )
     moves[0].start()
     for part in range(2):
 
@@ -428,6 +433,16 @@
 
         fetch(D3 + part * H, H, put_second)
     moves[1].start()
+    for base, count, target, move in (
+        (D3 + 2 * H, D2, nfirst_v, moves[2]),
+        (D3 + 2 * H + D2, D, nsecond_v, moves[3]),
+    ):
+
+        def put_node(done, take, side, value):
+            target[done : done + take, side * 128 : side * 128 + 128] = value
+
+        fetch(base, count, put_node)
+        move.start()
     row = 0
     for out in (v0, v1, v2, v3):
         for at in range(0, out.shape[1], 128):
@@ -443,58 +458,87 @@
     hbm = pl.BlockSpec(memory_space=pltpu.HBM)
     vm = pl.BlockSpec(memory_space=pltpu.VMEM)
     shapes = [(3 * D, H), (H, D)]
-    outs = shapes + [(1, H), (1, D), (1, D), (1, D)]
+    outs = shapes + [(1, H), (1, D), (1, D), (1, D), (2 * D, D), (D, D)]
+    held = shapes + [(2 * D, D // 2), (D, D // 2)]
     return pl.pallas_call(
         edge_out_kernel,
         out_shape=tuple(jax.ShapeDtypeStruct(s, F32) for s in outs),
         in_specs=[vm],
-        out_specs=(hbm, hbm, vm, vm, vm, vm),
-        scratch_shapes=[pltpu.VMEM(s, F32) for s in shapes] + [pltpu.SemaphoreType.DMA((2,))],
+        out_specs=(hbm, hbm, vm, vm, vm, vm, hbm, hbm),
+        scratch_shapes=[pltpu.VMEM(s, F32) for s in held] + [pltpu.SemaphoreType.DMA((4,))],
         compiler_params=pltpu.CompilerParams(vmem_limit_bytes=12 * 1024 * 1024),
-        cost_estimate=pl.CostEstimate(flops=1_000_000, bytes_accessed=3_000_000, transcendentals=0),
+        cost_estimate=pl.CostEstimate(flops=1_000_000, bytes_accessed=5_000_000, transcendentals=0),
         name="edge_out",
     )(full)
 
 
-def node_out_kernel(mine, other, first, second, first_v, second_v, sems):
+def node_out_kernel(other, first_in, second_in, first, second, first_v, second_v, sems):
     D2, D = first.shape
     half = D // 2
-    mine_at = own_columns(half)
-    other_at = pl.multiple_of(half - mine_at, half)
+    cols = pl.ds(pl.multiple_of(half - own_columns(half), half), half)
     skip = (3 * D + D2 // 2) % PIECE
-    last = mine.shape[0] // 2
-    moves = copies([(first_v, first), (second_v, second)], sems, 0)
+    last = other.shape[0] // 2
+    moves = copies([(first_v, first.at[:, cols]), (second_v, second.at[:, cols])], sems, 0)
     for base, count, out, move in ((0, D2, first_v, moves[0]), (D2, D, second_v, moves[1])):
-        for src, col in ((mine, mine_at), (other, other_at)):
-            done = 0
-            while done < count:
-                q, off = divmod(skip + base + done, PIECE)
-                take = min(count - done, PIECE - off)
-                for side in range(2):
-                    at = pl.ds(pl.multiple_of(col + side * 128, 128), 128)
-                    out[done : done + take, at] = src[q + last * side, off : off + take, :].astype(
-                        F32
-                    )
-                done += take
+        done = 0
+        while done < count:
+            q, off = divmod(skip + base + done, PIECE)
+            take = min(count - done, PIECE - off)
+            for side in range(2):
+                out[done : done + take, side * 128 : side * 128 + 128] = other[
+                    q + last * side, off : off + take, :
+                ].astype(F32)
+            done += take
         move.start()
     for m in moves:
         m.wait()
 
 
-def run_node_out(mine, other, D):
+def run_node_out(other, first, second):
     hbm = pl.BlockSpec(memory_space=pltpu.HBM)
     vm = pl.BlockSpec(memory_space=pltpu.VMEM)
-    shapes = [(2 * D, D), (D, D)]
+    shapes = [first.shape, second.shape]
     return pl.pallas_call(
         node_out_kernel,
         out_shape=tuple(jax.ShapeDtypeStruct(s, F32) for s in shapes),
-        in_specs=[vm, vm],
+        in_specs=[vm, hbm, hbm],
         out_specs=(hbm, hbm),
-        scratch_shapes=[pltpu.VMEM(s, F32) for s in shapes] + [pltpu.SemaphoreType.DMA((2,))],
+        input_output_aliases={1: 0, 2: 1},
+        scratch_shapes=[pltpu.VMEM((s[0], s[1] // 2), F32) for s in shapes]
+        + [pltpu.SemaphoreType.DMA((2,))],
         compiler_params=pltpu.CompilerParams(vmem_limit_bytes=12 * 1024 * 1024),
-        cost_estimate=pl.CostEstimate(flops=1_000_000, bytes_accessed=4_000_000, transcendentals=0),
+        cost_estimate=pl.CostEstimate(flops=1_000_000, bytes_accessed=2_000_000, transcendentals=0),
         name="node_out",
-    )(mine, other)
+    )(other, first, second)
+
+
+def sum_kernel(pieces, out):
+    def add(at):
+        total = pieces[0, at, :].astype(F32)
+        for p in range(1, pieces.shape[0]):
+            total = total + pieces[p, at, :].astype(F32)
+        out[at, :] = total.astype(BF)
+
+    step = 32
+
+    @pl.loop(0, PIECE // step)
+    def _(i):
+        add(pl.ds(pl.multiple_of(i * step, step), step))
+
+    add(slice(PIECE, PIECE + EXTRA))
+
+
+def run_sum(pieces):
+    vm = pl.BlockSpec(memory_space=pltpu.VMEM)
+    return pl.pallas_call(
+        sum_kernel,
+        out_shape=jax.ShapeDtypeStruct(pieces.shape[1:], BF),
+        in_specs=[vm],
+        out_specs=vm,
+        compiler_params=pltpu.CompilerParams(vmem_limit_bytes=4 * 1024 * 1024),
+        cost_estimate=pl.CostEstimate(flops=1_000_000, bytes_accessed=2_000_000, transcendentals=0),
+        name="sum_pieces",
+    )(pieces)
 
 
 def all_pieces(value, groups):
@@ -536,7 +580,7 @@
     from_prev = lax.ppermute(list1, "space", onward)
     from_next = lax.ppermute(list0, "space", backward)
 
-    grads, dh, u, ndx = run_layer(
+    ready = run_early(
         (
             senders[None],
             receivers[None],
@@ -553,27 +597,29 @@
             node_cotangent[0],
             edge_cotangent[0],
         ),
+        halo,
+    )
+    grads, gedges, gnodes, back_prev, back_next = run_layer(
+        ready,
         (from_prev, from_next, first_other, bias_other, second_other),
-    )
-    pieces = all_pieces(grads, PLANES)
-    gedges, gnodes, back_prev, back_next = run_inputs(
-        edge_first, edge_cotangent[0], node_cotangent[0], first_other, dh, u, ndx, halo
     )
     from_next = lax.ppermute(back_prev, "space", backward)
     from_prev = lax.ppermute(back_next, "space", onward)
-    pieces, from_next, from_prev = lax.optimization_barrier((pieces, from_next, from_prev))
-    part = jnp.sum(pieces.astype(F32), axis=0).astype(BF)
-    for bit in (2, 4):
-        near = lax.ppermute(part, ALL, across_z(bit))
-        part = (part.astype(F32) + near.astype(F32)).astype(BF)
-    full = all_pieces(jnp.broadcast_to(part[None], (GROUP, *part.shape)), PLANES)
+    pieces = all_pieces(grads, PLANES)
+    part = run_sum(pieces)
+    other = lax.ppermute(part, ALL, across_z(True))
+    part = (part.astype(F32) + other.astype(F32)).astype(BF)
+    other = lax.ppermute(part, ALL, across_z(False))
     grad_nodes = run_node(lists, gnodes, from_prev, from_next)
+    part = (part.astype(F32) + other.astype(F32)).astype(BF)
+    copied = jnp.broadcast_to(part[None], (GROUP, *part.shape))
+    full = all_pieces(copied, PLANES)
 
     split = (3 * D + 2 * H) // PIECE
     mine = full[2 * split :]
     other = lax.ppermute(mine, "hidden", swap)
-    edge_first_grad, edge_second_grad, v0, v1, v2, v3 = run_edge_out(full, D, H)
-    node_first_grad, node_second_grad = run_node_out(mine, other, D)
+    edge_first_grad, edge_second_grad, v0, v1, v2, v3, nfirst, nsecond = run_edge_out(full, D, H)
+    node_first_grad, node_second_grad = run_node_out(other, nfirst, nsecond)
     return (
         grad_nodes[None],
         gedges[None],

time: 114 us -> 113 us (level)
  blocking collectives: 26.7 us -> 56.4 us
  waiting for transfers between devices: 21.6 us -> 6.92 us
  starting transfers between devices: 39.5 us -> 31.2 us
  Pallas kernels: 23.2 us -> 17 us
  other arithmetic: 1.83 us -> 0.04 us
    all_to_all x1 -> x2, blocking collectives: 26.7 us -> 56.4 us  [all_pieces(): lax.all_to_all(value, ALL, 0, 0, axis_index_groups=groups, tiled=True)]
    ppermute x1, waiting for transfers between devices: 9.83 us -> 0.01 us  [step(): from_next = lax.ppermute(back_prev, 'space', backward)]
    all_to_all x1 -> x0, waiting for transfers between devices: 5.93 us -> none  [all_pieces(): lax.all_to_all(value, ALL, 0, 0, axis_index_groups=groups, tiled=True)]
    pallas_call x1, Pallas kernels: 13.5 us -> 7.62 us  [run_layer(): pl.pallas_call(layer_kernel, out_shape=(jax.ShapeDtypeStruct((GROUP, PIEC...]
    all_to_all x1 -> x0, starting transfers between devices: 4.74 us -> none  [all_pieces(): lax.all_to_all(value, ALL, 0, 0, axis_index_groups=groups, tiled=True)]
    ppermute x1, starting transfers between devices: 9.72 us -> 7.19 us  [step(): from_next = lax.ppermute(back_prev, 'space', backward)]
    reduce_sum x1 -> x0, other arithmetic: 1.79 us -> none  [step(): part = jnp.sum(pieces.astype(F32), axis=0).astype(BF)]
    ppermute x1, waiting for transfers between devices: 0.01 us -> 1.3 us  [step(): from_prev = lax.ppermute(back_next, 'space', onward)]
  transfers between devices with their start and end apart: 11 -> 10, of which waited for: 6 -> 3; matrix products, arithmetic and copies ran while one was open for 0% -> 0% of each run, Pallas kernels for 7% -> 7%
where the time goes in v1:
time: 113 us
  blocking collectives  56.4 us (50%)
  starting transfers between devices  31.2 us (28%)
  Pallas kernels  17 us (15%)
  waiting for transfers between devices  6.92 us (6%)
    all_to_all x2, blocking collectives, all_pieces(): lax.all_to_all(value, ALL, 0, 0, axis_index_groups=groups, tiled=True)  56.4 us
    ppermute x1, starting transfers between devices, step(): from_next = lax.ppermute(list0, 'space', backward)  8.77 us
    pallas_call x1, Pallas kernels, run_layer(): pl.pallas_call(layer_kernel, out_shape=(jax.ShapeDtypeStruct((GROUP, PIEC...  7.62 us
    ppermute x1, starting transfers between devices, step(): from_next = lax.ppermute(back_prev, 'space', backward)  7.19 us
    ppermute x1, starting transfers between devices, step(): other = lax.ppermute(mine, 'hidden', swap)  5.37 us
    ppermute x1, starting transfers between devices, step(): other = lax.ppermute(part, ALL, across_z(False))  5.07 us
    ppermute x1, waiting for transfers between devices, step(): other = lax.ppermute(part, ALL, across_z(True))  3.76 us
    ppermute x1, starting transfers between devices, step(): first_other = lax.ppermute(edge_first, 'hidden', swap)  3.29 us
  transfers between devices with their start and end apart: 10, of which 3 were waited for; matrix products, arithmetic and copies ran while one was open for 0% of the time, Pallas kernels for 7%

profile of v1, /device:TPU:1, one launch (start us, length us, event | category | flops | bytes accessed | tf_op | source)
XLA Modules:
  0.0 112.8 jit_solution(5873311697299987145)
XLA Ops:
  0.6 3.3 %collective-permute-start.2 = (bf16[1536,256]{1,0:T(8,128)(2,1)}, bf16[1536,256]{1,0:T(8,128)(2,1)S(1)}, u32[]{:S(2)}, u32[]{:S(2)}) collective-permute-start(bf16[1536,256]{1,0:T(8,128)(2,1)} %refs_3_.1), channel_id=1, source_target_pairs={{0,1},{1,0},{2,3},{3,2},{4,5},{5,4},{6,7},{7,6},{8,9},{9,8},{10,11... | collective-permute-start | bytes 2359304 | tf_op jit(solution)/shard_map/ppermute | solution.py:576
  3.9 0.1 collective-permute-start.4
  4.0 0.4 collective-permute-start.3
  4.4 1.2 %pick.1 = (bf16[64,512]{1,0:T(8,128)(2,1)S(1)}, bf16[64,512]{1,0:T(8,128)(2,1)S(1)}) custom-call(s32[2,64]{1,0:T(2,128)} %bitcast.32, bf16[128,512]{1,0:T(8,128)(2,1)} %bitcast.19), custom_call_target="tpu_custom_call" | custom-call | flops 200000000 | bytes 400000 | tf_op jit(solution)/shard_map/pick/pallas_call | solution.py:105
  5.6 0.1 collective-permute-start
  5.7 8.8 %collective-permute-start.1 = (bf16[64,512]{1,0:T(8,128)(2,1)S(1)}, bf16[64,512]{1,0:T(8,128)(2,1)S(1)}, u32[]{:S(2)}, u32[]{:S(2)}) collective-permute-start(bf16[64,512]{1,0:T(8,128)(2,1)S(1)} %get-tuple-element.56), channel_id=1, source_target_pairs={{2,0},{4,2},{6,4},{8,6},{10,8},{12,10},{14,12},{16,14},{18,16},{20... | collective-permute-start | bytes 196616 | tf_op jit(solution)/shard_map/ppermute | solution.py:581
  14.5 2.6 %early.1 = (bf16[128,512]{1,0:T(8,128)(2,1)S(1)}, bf16[1536,256]{1,0:T(8,128)(2,1)S(1)}, f32[1,256]{1,0:T(1,128)S(1)}, bf16[1024,512]{1,0:T(8,128)(2,1)S(1)}, bf...) custom-call(s32[1,1024]{1,0:T(1,128)} %bitcast.22, ...), custom_call_target="tpu_custom_call" | custom-call | flops 1500000000 | bytes 8000000 | tf_op jit(solution)/shard_map/early/pallas_call | solution.py:155
  17.1 0.0 collective-permute-done.3.refs_17_
  17.1 0.0 collective-permute-done.refs_14_
  17.1 0.0 collective-permute-done.1.refs_15_
  17.1 0.0 collective-permute-done.4.refs_18_
  17.1 0.0 collective-permute-done.2.refs_16_
  17.2 7.6 %layer.1 = (bf16[32,232,128]{2,1,0:T(8,128)(2,1)S(1)}, bf16[1024,256]{1,0:T(8,128)(2,1)}, f32[128,256]{1,0:T(8,128)S(1)}, bf16[64,256]{1,0:T(8,128)(2,1)S(1)}, bf16[64,256]{1,0:T(8,128)(2,1)S(1)}) custom-call(bf16[128,512]{1,0:T(8,128)(2,1)S(1)} %get-tuple-element.41.refs_0_, bf16[1536,256]{1,0:T(8,128)(2,1)S(1)} %get-tuple-element.42.refs_1_, ...), custom_call_target="tpu_custom_call" | custom-call | flops 6000000000 | bytes 12000000 | tf_op jit(solution)/shard_map/layer/pallas_call | solution.py:325
  24.8 29.4 %all_to_all.10.pieces = bf16[32,232,128]{2,1,0:T(8,128)(2,1)S(1)} all-to-all(bf16[32,232,128]{2,1,0:T(8,128)(2,1)S(1)} %get-tuple-element.61), channel_id=1, replica_groups={{0,2,128,130,16,18,144,146,32,34,160,162,48,50,176,178,64,66,192,194,80..., dimensions={0} | all-to-all | bytes 3801088 | tf_op jit(solution)/shard_map/all_to_all | solution.py:545
  54.2 0.3 sum_pieces.1
  54.6 0.9 collective-permute-start.7
  55.5 3.8 %collective-permute-done.7 = bf16[232,128]{1,0:T(8,128)(2,1)S(1)} collective-permute-done((bf16[232,128]{1,0:T(8,128)(2,1)S(1)}, bf16[232,128]{1,0:T(8,128)(2,1)S(1)}, u32[]{:S(2)}, u32[]{:S(2)}) %collective-permute-start.7) | collective-permute-done | bytes 59424 | tf_op jit(solution)/shard_map/ppermute | solution.py:610
  59.3 5.1 %collective-permute-start.8 = (bf16[232,128]{1,0:T(8,128)(2,1)S(1)}, bf16[232,128]{1,0:T(8,128)(2,1)S(1)}, u32[]{:S(2)}, u32[]{:S(2)}) collective-permute-start(bf16[232,128]{1,0:T(8,128)(2,1)S(1)} %add_convert_fusion.1), channel_id=1, source_target_pairs={{0,12},{1,13},{2,14},{3,15},{4,8},{5,9},{6,10},{7,11},{8,4},{9,5},... | collective-permute-start | bytes 178184 | tf_op jit(solution)/shard_map/ppermute | solution.py:612
  64.3 1.9 %collective-permute-done.8 = bf16[232,128]{1,0:T(8,128)(2,1)S(1)} collective-permute-done((bf16[232,128]{1,0:T(8,128)(2,1)S(1)}, bf16[232,128]{1,0:T(8,128)(2,1)S(1)}, u32[]{:S(2)}, u32[]{:S(2)}) %collective-permute-start.8) | collective-permute-done | bytes 59424 | tf_op jit(solution)/shard_map/ppermute | solution.py:612
  66.2 0.2 broadcast_in_dim.38
  66.5 27.0 %all_to_all.11.full = bf16[32,232,128]{2,1,0:T(8,128)(2,1)S(1)} all-to-all(bf16[32,232,128]{2,1,0:T(8,128)(2,1)S(1)} %broadcast_in_dim.38), channel_id=1, replica_groups={{0,2,128,130,16,18,144,146,32,34,160,162,48,50,176,178,64,66,192,194,80..., dimensions={0} | all-to-all | bytes 3801088 | tf_op jit(solution)/shard_map/all_to_all | solution.py:545
  93.5 0.1 slice.4
  93.5 5.4 %collective-permute-start.9 = (bf16[14,232,128]{2,1,0:T(8,128)(2,1)S(1)}, bf16[14,232,128]{2,1,0:T(8,128)(2,1)S(1)}, u32[]{:S(2)}, u32[]{:S(2)}) collective-permute-start(bf16[14,232,128]{2,1,0:T(8,128)(2,1)S(1)} %slice.4), channel_id=1, source_target_pairs={{0,1},{1,0},{2,3},{3,2},{4,5},{5,4},{6,7},{7,6},{8,9},{9,8},{10,11... | collective-permute-start | bytes 2494472 | tf_op jit(solution)/shard_map/ppermute | solution.py:620
  98.9 0.0 collective-permute-start.5
  98.9 7.2 %collective-permute-start.6 = (bf16[64,256]{1,0:T(8,128)(2,1)S(1)}, bf16[64,256]{1,0:T(8,128)(2,1)S(1)}, u32[]{:S(2)}, u32[]{:S(2)}) collective-permute-start(bf16[64,256]{1,0:T(8,128)(2,1)S(1)} %get-tuple-element.59), channel_id=1, source_target_pairs={{2,0},{4,2},{6,4},{8,6},{10,8},{12,10},{14,12},{16,14},{18,16},{20... | collective-permute-start | bytes 98312 | tf_op jit(solution)/shard_map/ppermute | solution.py:606
  106.1 1.3 %collective-permute-done.5.first = bf16[64,256]{1,0:T(8,128)(2,1)S(1)} collective-permute-done((bf16[64,256]{1,0:T(8,128)(2,1)S(1)}, bf16[64,256]{1,0:T(8,128)(2,1)S(1)}, u32[]{:S(2)}, u32[]{:S(2)}) %collective-permute-start.5) | collective-permute-done | bytes 32800 | tf_op jit(solution)/shard_map/ppermute | solution.py:607
  107.4 0.0 collective-permute-done.6.second
  107.4 1.5 %node_gradient.1 = bf16[128,256]{1,0:T(8,128)(2,1)} custom-call(s32[2,64]{1,0:T(2,128)} %bitcast.33, f32[128,256]{1,0:T(8,128)S(1)} %get-tuple-element.57.gnodes, bf16[64,256]{1,0:T(8,128)(2,1)S(1)} %collective-permute-done.5.first, bf16[64,256]{1,0:T(8,128)(2,1)S(1)} %collective-permute-done.6.second), custom_call_target="tpu_custom_call" | custom-call | flops 100000000 | bytes 300000 | tf_op jit(solution)/shard_map/node_gradient/pallas_call | solution.py:377
  108.9 2.6 %edge_out.1 = (f32[1536,256]{1,0:T(8,128)}, f32[256,512]{1,0:T(8,128)}, f32[1,256]{1,0:T(1,128)}, f32[1,512]{1,0:T(1,128)}, f32[1,512]{1,0:T(1,128)}, /*index=5*...) custom-call(bf16[32,232,128]{2,1,0:T(8,128)(2,1)S(1)} %all_to_all.11.full), custom_call_target="tpu_custom_call" | custom-call | flops 1000000 | bytes 5000000 | tf_op jit(solution)/shard_map/edge_out/pallas_call | solution.py:463
  111.4 0.0 collective-permute-done.9.other
  111.4 1.2 %node_out.1 = (f32[1024,512]{1,0:T(8,128)}, f32[512,512]{1,0:T(8,128)}) custom-call(bf16[14,232,128]{2,1,0:T(8,128)(2,1)S(1)} %collective-permute-done.9.other, f32[1024,512]{1,0:T(8,128)} %get-tuple-element.66.first_in, f32[512,512]{1,0:T(8,128)} %get-tuple-element.67.second_in), custom_call_target="tpu_custom_call", output_to_operand_aliasing={{0}: (1, {}), {1}: (2, {})} | custom-call | flops 1000000 | bytes 2000000 | tf_op jit(solution)/shard_map/node_out/pallas_call | solution.py:501
  (2 shorter events, 0.0 us)
Async XLA Ops:
  0.6 16.5 %collective-permute-start.2 = (bf16[1536,256]{1,0:T(8,128)(2,1)}, bf16[1536,256]{1,0:T(8,128)(2,1)S(1)}, u32[]{:S(2)}, u32[]{:S(2)}) collective-permute-start(bf16[1536,256]{1,0:T(8,128)(2,1)} %refs_3_.1), channel_id=1, source_target_pairs={{0,1},{1,0},{2,3},{3,2},{4,5},{5,4},{6,7},{7,6},{8,9},{9,8},{10,11... | collective-permute-start | bytes 2359304 | tf_op jit(solution)/shard_map/ppermute | solution.py:576
  3.9 13.2 %collective-permute-start.4 = (bf16[256,512]{1,0:T(8,128)(2,1)}, bf16[256,512]{1,0:T(8,128)(2,1)S(1)}, u32[]{:S(2)}, u32[]{:S(2)}) collective-permute-start(bf16[256,512]{1,0:T(8,128)(2,1)} %refs_6_.1), channel_id=1, source_target_pairs={{0,1},{1,0},{2,3},{3,2},{4,5},{5,4},{6,7},{7,6},{8,9},{9,8},{10,11... | collective-permute-start | bytes 786440 | tf_op jit(solution)/shard_map/ppermute | solution.py:577
  4.0 13.1 %collective-permute-start.3 = (f32[1,256]{1,0:T(1,128)}, f32[1,256]{1,0:T(1,128)S(1)}, u32[]{:S(2)}, u32[]{:S(2)}) collective-permute-start(f32[1,256]{1,0:T(1,128)} %bitcast.30), channel_id=1, source_target_pairs={{0,1},{1,0},{2,3},{3,2},{4,5},{5,4},{6,7},{7,6},{8,9},{9,8},{10,11... | collective-permute-start | bytes 3080 | tf_op jit(solution)/shard_map/ppermute | solution.py:578
  5.6 11.5 %collective-permute-start = (bf16[64,512]{1,0:T(8,128)(2,1)S(1)}, bf16[64,512]{1,0:T(8,128)(2,1)S(1)}, u32[]{:S(2)}, u32[]{:S(2)}) collective-permute-start(bf16[64,512]{1,0:T(8,128)(2,1)S(1)} %get-tuple-element.55), channel_id=1, source_target_pairs={{0,2},{2,4},{4,6},{6,8},{8,10},{10,12},{12,14},{14,16},{16,18},{18... | collective-permute-start | bytes 196616 | tf_op jit(solution)/shard_map/ppermute | solution.py:580
  5.7 11.4 %collective-permute-start.1 = (bf16[64,512]{1,0:T(8,128)(2,1)S(1)}, bf16[64,512]{1,0:T(8,128)(2,1)S(1)}, u32[]{:S(2)}, u32[]{:S(2)}) collective-permute-start(bf16[64,512]{1,0:T(8,128)(2,1)S(1)} %get-tuple-element.56), channel_id=1, source_target_pairs={{2,0},{4,2},{6,4},{8,6},{10,8},{12,10},{14,12},{16,14},{18,16},{20... | collective-permute-start | bytes 196616 | tf_op jit(solution)/shard_map/ppermute | solution.py:581
  54.6 4.7 %collective-permute-start.7 = (bf16[232,128]{1,0:T(8,128)(2,1)S(1)}, bf16[232,128]{1,0:T(8,128)(2,1)S(1)}, u32[]{:S(2)}, u32[]{:S(2)}) collective-permute-start(bf16[232,128]{1,0:T(8,128)(2,1)S(1)} %sum_pieces.1), channel_id=1, source_target_pairs={{0,4},{1,5},{2,6},{3,7},{4,0},{5,1},{6,2},{7,3},{8,12},{9,13},{10,... | collective-permute-start | bytes 178184 | tf_op jit(solution)/shard_map/ppermute | solution.py:610
  59.3 6.9 %collective-permute-start.8 = (bf16[232,128]{1,0:T(8,128)(2,1)S(1)}, bf16[232,128]{1,0:T(8,128)(2,1)S(1)}, u32[]{:S(2)}, u32[]{:S(2)}) collective-permute-start(bf16[232,128]{1,0:T(8,128)(2,1)S(1)} %add_convert_fusion.1), channel_id=1, source_target_pairs={{0,12},{1,13},{2,14},{3,15},{4,8},{5,9},{6,10},{7,11},{8,4},{9,5},... | collective-permute-start | bytes 178184 | tf_op jit(solution)/shard_map/ppermute | solution.py:612
  93.5 17.9 %collective-permute-start.9 = (bf16[14,232,128]{2,1,0:T(8,128)(2,1)S(1)}, bf16[14,232,128]{2,1,0:T(8,128)(2,1)S(1)}, u32[]{:S(2)}, u32[]{:S(2)}) collective-permute-start(bf16[14,232,128]{2,1,0:T(8,128)(2,1)S(1)} %slice.4), channel_id=1, source_target_pairs={{0,1},{1,0},{2,3},{3,2},{4,5},{5,4},{6,7},{7,6},{8,9},{9,8},{10,11... | collective-permute-start | bytes 2494472 | tf_op jit(solution)/shard_map/ppermute | solution.py:620
  98.9 8.5 %collective-permute-start.5 = (bf16[64,256]{1,0:T(8,128)(2,1)S(1)}, bf16[64,256]{1,0:T(8,128)(2,1)S(1)}, u32[]{:S(2)}, u32[]{:S(2)}) collective-permute-start(bf16[64,256]{1,0:T(8,128)(2,1)S(1)} %get-tuple-element.58), channel_id=1, source_target_pairs={{0,2},{2,4},{4,6},{6,8},{8,10},{10,12},{12,14},{14,16},{16,18},{18... | collective-permute-start | bytes 98312 | tf_op jit(solution)/shard_map/ppermute | solution.py:607
  98.9 8.5 %collective-permute-start.6 = (bf16[64,256]{1,0:T(8,128)(2,1)S(1)}, bf16[64,256]{1,0:T(8,128)(2,1)S(1)}, u32[]{:S(2)}, u32[]{:S(2)}) collective-permute-start(bf16[64,256]{1,0:T(8,128)(2,1)S(1)} %get-tuple-element.59), channel_id=1, source_target_pairs={{2,0},{4,2},{6,4},{8,6},{10,8},{12,10},{14,12},{16,14},{18,16},{20... | collective-permute-start | bytes 98312 | tf_op jit(solution)/shard_map/ppermute | solution.py:606

commit v2 on v1

--- a/solution.py
+++ b/solution.py
@@ -359,36 +359,30 @@
     )(*params, *arrived)
 
 
-def node_kernel(lists, gnodes, first, second, out, lists_v, sems):
-    move = pltpu.make_async_copy(lists, lists_v, sems.at[0])
-    move.start()
-    move.wait()
-    N, K = gnodes.shape[0], first.shape[0]
-    total = gnodes[...]
-    for i, value in enumerate((first, second)):
-        hot = lax.broadcasted_iota(jnp.int32, (N, K), 0) == lists_v[i : i + 1, :]
-        total = total + dot(hot.astype(F32).astype(BF), value[...])
-    out[...] = total.astype(BF)
-
-
-def run_node(lists, gnodes, first, second):
-    hbm = pl.BlockSpec(memory_space=pltpu.HBM)
-    vm = pl.BlockSpec(memory_space=pltpu.VMEM)
-    return pl.pallas_call(
-        node_kernel,
-        out_shape=jax.ShapeDtypeStruct(gnodes.shape, BF),
-        in_specs=[hbm, vm, vm, vm],
-        out_specs=vm,
-        scratch_shapes=[pltpu.VMEM(lists.shape, jnp.int32), pltpu.SemaphoreType.DMA((1,))],
-        compiler_params=pltpu.CompilerParams(vmem_limit_bytes=4 * 1024 * 1024),
-        cost_estimate=pl.CostEstimate(flops=100_000_000, bytes_accessed=300_000, transcendentals=0),
-        name="node_gradient",
-    )(*in_hbm(lists), gnodes, first, second)
-
-
 def edge_out_kernel(
-    full, first, second, v0, v1, v2, v3, nfirst, nsecond, first_v, second_v, nfirst_v, nsecond_v, sems
+    full,
+    lists,
+    gnodes,
+    back_p,
+    back_n,
+    first,
+    second,
+    v0,
+    v1,
+    v2,
+    v3,
+    nfirst,
+    nsecond,
+    gout,
+    first_v,
+    second_v,
+    nfirst_v,
+    nsecond_v,
+    lists_v,
+    sems,
 ):
+    asked = pltpu.make_async_copy(lists, lists_v, sems.at[4])
+    asked.start()
     D3, _ = first.shape
     H = second.shape[0]
     half = second.shape[1] // 2
@@ -450,11 +444,18 @@
             tile = full[piece, PIECE:, :].astype(F32)
             out[:, at : at + 128] = tile[off : off + 1, :]
             row += 1
+    asked.wait()
+    N, K = gnodes.shape[0], back_p.shape[0]
+    total = gnodes[...]
+    for i, value in enumerate((back_p, back_n)):
+        hot = lax.broadcasted_iota(jnp.int32, (N, K), 0) == lists_v[i : i + 1, :]
+        total = total + dot(hot.astype(F32).astype(BF), value[...])
+    gout[...] = total.astype(BF)
     for m in moves:
         m.wait()
 
 
-def run_edge_out(full, D, H):
+def run_edge_out(full, lists, gnodes, back_p, back_n, D, H):
     hbm = pl.BlockSpec(memory_space=pltpu.HBM)
     vm = pl.BlockSpec(memory_space=pltpu.VMEM)
     shapes = [(3 * D, H), (H, D)]
@@ -462,14 +463,16 @@
     held = shapes + [(2 * D, D // 2), (D, D // 2)]
     return pl.pallas_call(
         edge_out_kernel,
-        out_shape=tuple(jax.ShapeDtypeStruct(s, F32) for s in outs),
-        in_specs=[vm],
-        out_specs=(hbm, hbm, vm, vm, vm, vm, hbm, hbm),
-        scratch_shapes=[pltpu.VMEM(s, F32) for s in held] + [pltpu.SemaphoreType.DMA((4,))],
+        out_shape=tuple(jax.ShapeDtypeStruct(s, F32) for s in outs)
+        + (jax.ShapeDtypeStruct(gnodes.shape, BF),),
+        in_specs=[vm, hbm, vm, vm, vm],
+        out_specs=(hbm, hbm, vm, vm, vm, vm, hbm, hbm, vm),
+        scratch_shapes=[pltpu.VMEM(s, F32) for s in held]
+        + [pltpu.VMEM(lists.shape, jnp.int32), pltpu.SemaphoreType.DMA((5,))],
         compiler_params=pltpu.CompilerParams(vmem_limit_bytes=12 * 1024 * 1024),
         cost_estimate=pl.CostEstimate(flops=1_000_000, bytes_accessed=5_000_000, transcendentals=0),
         name="edge_out",
-    )(full)
+    )(full, *in_hbm(lists), gnodes, back_p, back_n)
 
 
 def node_out_kernel(other, first_in, second_in, first, second, first_v, second_v, sems):
@@ -610,7 +613,6 @@
     other = lax.ppermute(part, ALL, across_z(True))
     part = (part.astype(F32) + other.astype(F32)).astype(BF)
     other = lax.ppermute(part, ALL, across_z(False))
-    grad_nodes = run_node(lists, gnodes, from_prev, from_next)
     part = (part.astype(F32) + other.astype(F32)).astype(BF)
     copied = jnp.broadcast_to(part[None], (GROUP, *part.shape))
     full = all_pieces(copied, PLANES)
@@ -618,7 +620,9 @@
     split = (3 * D + 2 * H) // PIECE
     mine = full[2 * split :]
     other = lax.ppermute(mine, "hidden", swap)
-    edge_first_grad, edge_second_grad, v0, v1, v2, v3, nfirst, nsecond = run_edge_out(full, D, H)
+    (edge_first_grad, edge_second_grad, v0, v1, v2, v3, nfirst, nsecond, grad_nodes) = run_edge_out(
+        full, lists, gnodes, from_prev, from_next, D, H
+    )
     node_first_grad, node_second_grad = run_node_out(other, nfirst, nsecond)
     return (
         grad_nodes[None],

time: 113 us -> 112 us (level)
  Pallas kernels: 17 us -> 15.6 us
    pallas_call x1 -> x0, Pallas kernels: 1.49 us -> none  [run_node(): pl.pallas_call(node_kernel, out_shape=jax.ShapeDtypeStruct(gnodes.shape,...]
  transfers between devices with their start and end apart: 10 -> 10, of which waited for: 3 -> 3; matrix products, arithmetic and copies ran while one was open for 0% -> 0% of each run, Pallas kernels for 7% -> 6%
where the time goes in v2:
time: 112 us; the launch traced here: 111 us
  blocking collectives  56.4 us (50%)
  starting transfers between devices  31.2 us (28%)
  Pallas kernels  15.6 us (14%)
  waiting for transfers between devices  6.92 us (6%)
    all_to_all x2, blocking collectives, all_pieces(): lax.all_to_all(value, ALL, 0, 0, axis_index_groups=groups, tiled=True)  56.4 us
    ppermute x1, starting transfers between devices, step(): from_next = lax.ppermute(list0, 'space', backward)  8.77 us
    pallas_call x1, Pallas kernels, run_layer(): pl.pallas_call(layer_kernel, out_shape=(jax.ShapeDtypeStruct((GROUP, PIEC...  7.62 us
    ppermute x1, starting transfers between devices, step(): from_next = lax.ppermute(back_prev, 'space', backward)  7.19 us
    ppermute x1, starting transfers between devices, step(): other = lax.ppermute(mine, 'hidden', swap)  5.37 us
    ppermute x1, starting transfers between devices, step(): other = lax.ppermute(part, ALL, across_z(False))  5.07 us
    ppermute x1, waiting for transfers between devices, step(): other = lax.ppermute(part, ALL, across_z(True))  3.76 us
    ppermute x1, starting transfers between devices, step(): first_other = lax.ppermute(edge_first, 'hidden', swap)  3.29 us
  transfers between devices with their start and end apart: 10, of which 3 were waited for; matrix products, arithmetic and copies ran while one was open for 0% of the time, Pallas kernels for 6%

profile of v2, /device:TPU:1, one launch (start us, length us, event | category | flops | bytes accessed | tf_op | source)
XLA Modules:
  0.0 111.4 jit_solution(12556306690870302982)
XLA Ops:
  0.6 3.3 %collective-permute-start.2 = (bf16[1536,256]{1,0:T(8,128)(2,1)}, bf16[1536,256]{1,0:T(8,128)(2,1)S(1)}, u32[]{:S(2)}, u32[]{:S(2)}) collective-permute-start(bf16[1536,256]{1,0:T(8,128)(2,1)} %refs_3_.1), channel_id=1, source_target_pairs={{0,1},{1,0},{2,3},{3,2},{4,5},{5,4},{6,7},{7,6},{8,9},{9,8},{10,11... | collective-permute-start | bytes 2359304 | tf_op jit(solution)/shard_map/ppermute | solution.py:579
  3.9 0.1 collective-permute-start.4
  4.0 0.4 collective-permute-start.3
  4.4 1.2 %pick.1 = (bf16[64,512]{1,0:T(8,128)(2,1)S(1)}, bf16[64,512]{1,0:T(8,128)(2,1)S(1)}) custom-call(s32[2,64]{1,0:T(2,128)} %bitcast.17, bf16[128,512]{1,0:T(8,128)(2,1)} %bitcast.21), custom_call_target="tpu_custom_call" | custom-call | flops 200000000 | bytes 400000 | tf_op jit(solution)/shard_map/pick/pallas_call | solution.py:105
  5.6 0.1 collective-permute-start
  5.7 8.8 %collective-permute-start.1 = (bf16[64,512]{1,0:T(8,128)(2,1)S(1)}, bf16[64,512]{1,0:T(8,128)(2,1)S(1)}, u32[]{:S(2)}, u32[]{:S(2)}) collective-permute-start(bf16[64,512]{1,0:T(8,128)(2,1)S(1)} %get-tuple-element.57), channel_id=1, source_target_pairs={{2,0},{4,2},{6,4},{8,6},{10,8},{12,10},{14,12},{16,14},{18,16},{20... | collective-permute-start | bytes 196616 | tf_op jit(solution)/shard_map/ppermute | solution.py:584
  14.5 2.6 %early.1 = (bf16[128,512]{1,0:T(8,128)(2,1)S(1)}, bf16[1536,256]{1,0:T(8,128)(2,1)S(1)}, f32[1,256]{1,0:T(1,128)S(1)}, bf16[1024,512]{1,0:T(8,128)(2,1)S(1)}, bf...) custom-call(s32[1,1024]{1,0:T(1,128)} %bitcast.25, ...), custom_call_target="tpu_custom_call" | custom-call | flops 1500000000 | bytes 8000000 | tf_op jit(solution)/shard_map/early/pallas_call | solution.py:155
  17.1 0.0 collective-permute-done.3.refs_17_
  17.1 0.0 collective-permute-done.refs_14_
  17.1 0.0 collective-permute-done.1.refs_15_
  17.1 0.0 collective-permute-done.4.refs_18_
  17.1 0.0 collective-permute-done.2.refs_16_
  17.2 7.6 %layer.1 = (bf16[32,232,128]{2,1,0:T(8,128)(2,1)S(1)}, bf16[1024,256]{1,0:T(8,128)(2,1)}, f32[128,256]{1,0:T(8,128)S(1)}, bf16[64,256]{1,0:T(8,128)(2,1)S(1)}, bf16[64,256]{1,0:T(8,128)(2,1)S(1)}) custom-call(bf16[128,512]{1,0:T(8,128)(2,1)S(1)} %get-tuple-element.42.refs_0_, bf16[1536,256]{1,0:T(8,128)(2,1)S(1)} %get-tuple-element.43.refs_1_, ...), custom_call_target="tpu_custom_call" | custom-call | flops 6000000000 | bytes 12000000 | tf_op jit(solution)/shard_map/layer/pallas_call | solution.py:325
  24.8 29.4 %all_to_all.10.pieces = bf16[32,232,128]{2,1,0:T(8,128)(2,1)S(1)} all-to-all(bf16[32,232,128]{2,1,0:T(8,128)(2,1)S(1)} %get-tuple-element.58), channel_id=1, replica_groups={{0,2,128,130,16,18,144,146,32,34,160,162,48,50,176,178,64,66,192,194,80..., dimensions={0} | all-to-all | bytes 3801088 | tf_op jit(solution)/shard_map/all_to_all | solution.py:548
  54.2 0.3 sum_pieces.1
  54.6 0.9 collective-permute-start.5
  55.5 3.8 %collective-permute-done.5 = bf16[232,128]{1,0:T(8,128)(2,1)S(1)} collective-permute-done((bf16[232,128]{1,0:T(8,128)(2,1)S(1)}, bf16[232,128]{1,0:T(8,128)(2,1)S(1)}, u32[]{:S(2)}, u32[]{:S(2)}) %collective-permute-start.5) | collective-permute-done | bytes 59424 | tf_op jit(solution)/shard_map/ppermute | solution.py:613
  59.3 5.1 %collective-permute-start.6 = (bf16[232,128]{1,0:T(8,128)(2,1)S(1)}, bf16[232,128]{1,0:T(8,128)(2,1)S(1)}, u32[]{:S(2)}, u32[]{:S(2)}) collective-permute-start(bf16[232,128]{1,0:T(8,128)(2,1)S(1)} %add_convert_fusion.1), channel_id=1, source_target_pairs={{0,12},{1,13},{2,14},{3,15},{4,8},{5,9},{6,10},{7,11},{8,4},{9,5},... | collective-permute-start | bytes 178184 | tf_op jit(solution)/shard_map/ppermute | solution.py:615
  64.3 1.9 %collective-permute-done.6 = bf16[232,128]{1,0:T(8,128)(2,1)S(1)} collective-permute-done((bf16[232,128]{1,0:T(8,128)(2,1)S(1)}, bf16[232,128]{1,0:T(8,128)(2,1)S(1)}, u32[]{:S(2)}, u32[]{:S(2)}) %collective-permute-start.6) | collective-permute-done | bytes 59424 | tf_op jit(solution)/shard_map/ppermute | solution.py:615
  66.2 0.2 broadcast_in_dim.36
  66.5 27.0 %all_to_all.11.full = bf16[32,232,128]{2,1,0:T(8,128)(2,1)S(1)} all-to-all(bf16[32,232,128]{2,1,0:T(8,128)(2,1)S(1)} %broadcast_in_dim.36), channel_id=1, replica_groups={{0,2,128,130,16,18,144,146,32,34,160,162,48,50,176,178,64,66,192,194,80..., dimensions={0} | all-to-all | bytes 3801088 | tf_op jit(solution)/shard_map/all_to_all | solution.py:548
  93.5 0.1 slice.4
  93.5 5.4 %collective-permute-start.9 = (bf16[14,232,128]{2,1,0:T(8,128)(2,1)S(1)}, bf16[14,232,128]{2,1,0:T(8,128)(2,1)S(1)}, u32[]{:S(2)}, u32[]{:S(2)}) collective-permute-start(bf16[14,232,128]{2,1,0:T(8,128)(2,1)S(1)} %slice.4), channel_id=1, source_target_pairs={{0,1},{1,0},{2,3},{3,2},{4,5},{5,4},{6,7},{7,6},{8,9},{9,8},{10,11... | collective-permute-start | bytes 2494472 | tf_op jit(solution)/shard_map/ppermute | solution.py:622
  98.9 0.0 collective-permute-start.7
  98.9 7.2 %collective-permute-start.8 = (bf16[64,256]{1,0:T(8,128)(2,1)S(1)}, bf16[64,256]{1,0:T(8,128)(2,1)S(1)}, u32[]{:S(2)}, u32[]{:S(2)}) collective-permute-start(bf16[64,256]{1,0:T(8,128)(2,1)S(1)} %get-tuple-element.61), channel_id=1, source_target_pairs={{2,0},{4,2},{6,4},{8,6},{10,8},{12,10},{14,12},{16,14},{18,16},{20... | collective-permute-start | bytes 98312 | tf_op jit(solution)/shard_map/ppermute | solution.py:609
  106.1 1.3 %collective-permute-done.7.back_p = bf16[64,256]{1,0:T(8,128)(2,1)S(1)} collective-permute-done((bf16[64,256]{1,0:T(8,128)(2,1)S(1)}, bf16[64,256]{1,0:T(8,128)(2,1)S(1)}, u32[]{:S(2)}, u32[]{:S(2)}) %collective-permute-start.7) | collective-permute-done | bytes 32800 | tf_op jit(solution)/shard_map/ppermute | solution.py:610
  107.4 0.0 collective-permute-done.8.back_n
  107.4 2.6 %edge_out.1 = (f32[1536,256]{1,0:T(8,128)}, f32[256,512]{1,0:T(8,128)}, f32[1,256]{1,0:T(1,128)}, f32[1,512]{1,0:T(1,128)}, f32[1,512]{1,0:T(1,128)}, /*index=5*...) custom-call(bf16[32,232,128]{2,1,0:T(8,128)(2,1)S(1)} %all_to_all.11.full, ...), custom_call_target="tpu_custom_call" | custom-call | flops 1000000 | bytes 5000000 | tf_op jit(solution)/shard_map/edge_out/pallas_call | solution.py:464
  110.0 0.0 collective-permute-done.9.other
  110.0 1.2 %node_out.1 = (f32[1024,512]{1,0:T(8,128)}, f32[512,512]{1,0:T(8,128)}) custom-call(bf16[14,232,128]{2,1,0:T(8,128)(2,1)S(1)} %collective-permute-done.9.other, f32[1024,512]{1,0:T(8,128)} %get-tuple-element.68.first_in, f32[512,512]{1,0:T(8,128)} %get-tuple-element.69.second_in), custom_call_target="tpu_custom_call", output_to_operand_aliasing={{0}: (1, {}), {1}: (2, {})} | custom-call | flops 1000000 | bytes 2000000 | tf_op jit(solution)/shard_map/node_out/pallas_call | solution.py:504
  (2 shorter events, 0.0 us)
Async XLA Ops:
  0.6 16.5 %collective-permute-start.2 = (bf16[1536,256]{1,0:T(8,128)(2,1)}, bf16[1536,256]{1,0:T(8,128)(2,1)S(1)}, u32[]{:S(2)}, u32[]{:S(2)}) collective-permute-start(bf16[1536,256]{1,0:T(8,128)(2,1)} %refs_3_.1), channel_id=1, source_target_pairs={{0,1},{1,0},{2,3},{3,2},{4,5},{5,4},{6,7},{7,6},{8,9},{9,8},{10,11... | collective-permute-start | bytes 2359304 | tf_op jit(solution)/shard_map/ppermute | solution.py:579
  3.9 13.2 %collective-permute-start.4 = (bf16[256,512]{1,0:T(8,128)(2,1)}, bf16[256,512]{1,0:T(8,128)(2,1)S(1)}, u32[]{:S(2)}, u32[]{:S(2)}) collective-permute-start(bf16[256,512]{1,0:T(8,128)(2,1)} %refs_6_.1), channel_id=1, source_target_pairs={{0,1},{1,0},{2,3},{3,2},{4,5},{5,4},{6,7},{7,6},{8,9},{9,8},{10,11... | collective-permute-start | bytes 786440 | tf_op jit(solution)/shard_map/ppermute | solution.py:580
  4.0 13.1 %collective-permute-start.3 = (f32[1,256]{1,0:T(1,128)}, f32[1,256]{1,0:T(1,128)S(1)}, u32[]{:S(2)}, u32[]{:S(2)}) collective-permute-start(f32[1,256]{1,0:T(1,128)} %bitcast.33), channel_id=1, source_target_pairs={{0,1},{1,0},{2,3},{3,2},{4,5},{5,4},{6,7},{7,6},{8,9},{9,8},{10,11... | collective-permute-start | bytes 3080 | tf_op jit(solution)/shard_map/ppermute | solution.py:581
  5.6 11.5 %collective-permute-start = (bf16[64,512]{1,0:T(8,128)(2,1)S(1)}, bf16[64,512]{1,0:T(8,128)(2,1)S(1)}, u32[]{:S(2)}, u32[]{:S(2)}) collective-permute-start(bf16[64,512]{1,0:T(8,128)(2,1)S(1)} %get-tuple-element.56), channel_id=1, source_target_pairs={{0,2},{2,4},{4,6},{6,8},{8,10},{10,12},{12,14},{14,16},{16,18},{18... | collective-permute-start | bytes 196616 | tf_op jit(solution)/shard_map/ppermute | solution.py:583
  5.7 11.4 %collective-permute-start.1 = (bf16[64,512]{1,0:T(8,128)(2,1)S(1)}, bf16[64,512]{1,0:T(8,128)(2,1)S(1)}, u32[]{:S(2)}, u32[]{:S(2)}) collective-permute-start(bf16[64,512]{1,0:T(8,128)(2,1)S(1)} %get-tuple-element.57), channel_id=1, source_target_pairs={{2,0},{4,2},{6,4},{8,6},{10,8},{12,10},{14,12},{16,14},{18,16},{20... | collective-permute-start | bytes 196616 | tf_op jit(solution)/shard_map/ppermute | solution.py:584
  54.6 4.7 %collective-permute-start.5 = (bf16[232,128]{1,0:T(8,128)(2,1)S(1)}, bf16[232,128]{1,0:T(8,128)(2,1)S(1)}, u32[]{:S(2)}, u32[]{:S(2)}) collective-permute-start(bf16[232,128]{1,0:T(8,128)(2,1)S(1)} %sum_pieces.1), channel_id=1, source_target_pairs={{0,4},{1,5},{2,6},{3,7},{4,0},{5,1},{6,2},{7,3},{8,12},{9,13},{10,... | collective-permute-start | bytes 178184 | tf_op jit(solution)/shard_map/ppermute | solution.py:613
  59.3 6.9 %collective-permute-start.6 = (bf16[232,128]{1,0:T(8,128)(2,1)S(1)}, bf16[232,128]{1,0:T(8,128)(2,1)S(1)}, u32[]{:S(2)}, u32[]{:S(2)}) collective-permute-start(bf16[232,128]{1,0:T(8,128)(2,1)S(1)} %add_convert_fusion.1), channel_id=1, source_target_pairs={{0,12},{1,13},{2,14},{3,15},{4,8},{5,9},{6,10},{7,11},{8,4},{9,5},... | collective-permute-start | bytes 178184 | tf_op jit(solution)/shard_map/ppermute | solution.py:615
  93.5 16.5 %collective-permute-start.9 = (bf16[14,232,128]{2,1,0:T(8,128)(2,1)S(1)}, bf16[14,232,128]{2,1,0:T(8,128)(2,1)S(1)}, u32[]{:S(2)}, u32[]{:S(2)}) collective-permute-start(bf16[14,232,128]{2,1,0:T(8,128)(2,1)S(1)} %slice.4), channel_id=1, source_target_pairs={{0,1},{1,0},{2,3},{3,2},{4,5},{5,4},{6,7},{7,6},{8,9},{9,8},{10,11... | collective-permute-start | bytes 2494472 | tf_op jit(solution)/shard_map/ppermute | solution.py:622
  98.9 8.5 %collective-permute-start.7 = (bf16[64,256]{1,0:T(8,128)(2,1)S(1)}, bf16[64,256]{1,0:T(8,128)(2,1)S(1)}, u32[]{:S(2)}, u32[]{:S(2)}) collective-permute-start(bf16[64,256]{1,0:T(8,128)(2,1)S(1)} %get-tuple-element.60), channel_id=1, source_target_pairs={{0,2},{2,4},{4,6},{6,8},{8,10},{10,12},{12,14},{14,16},{16,18},{18... | collective-permute-start | bytes 98312 | tf_op jit(solution)/shard_map/ppermute | solution.py:610
  98.9 8.5 %collective-permute-start.8 = (bf16[64,256]{1,0:T(8,128)(2,1)S(1)}, bf16[64,256]{1,0:T(8,128)(2,1)S(1)}, u32[]{:S(2)}, u32[]{:S(2)}) collective-permute-start(bf16[64,256]{1,0:T(8,128)(2,1)S(1)} %get-tuple-element.61), channel_id=1, source_target_pairs={{2,0},{4,2},{6,4},{8,6},{10,8},{12,10},{14,12},{16,14},{18,16},{20... | collective-permute-start | bytes 98312 | tf_op jit(solution)/shard_map/ppermute | solution.py:609

commit v3 on v2

--- a/solution.py
+++ b/solution.py
@@ -544,6 +544,25 @@
     )(pieces)
 
 
+def spread_kernel(part, other, out):
+    total = (part[...].astype(F32) + other[...].astype(F32)).astype(BF)
+    for piece in range(out.shape[0]):
+        out[piece, :, :] = total
+
+
+def run_spread(part, other):
+    vm = pl.BlockSpec(memory_space=pltpu.VMEM)
+    return pl.pallas_call(
+        spread_kernel,
+        out_shape=jax.ShapeDtypeStruct((GROUP, *part.shape), BF),
+        in_specs=[vm, vm],
+        out_specs=vm,
+        compiler_params=pltpu.CompilerParams(vmem_limit_bytes=4 * 1024 * 1024),
+        cost_estimate=pl.CostEstimate(flops=1_000_000, bytes_accessed=2_000_000, transcendentals=0),
+        name="spread",
+    )(part, other)
+
+
 def all_pieces(value, groups):
     return lax.all_to_all(value, ALL, 0, 0, axis_index_groups=groups, tiled=True)
 
@@ -613,8 +632,7 @@
     other = lax.ppermute(part, ALL, across_z(True))
     part = (part.astype(F32) + other.astype(F32)).astype(BF)
     other = lax.ppermute(part, ALL, across_z(False))
-    part = (part.astype(F32) + other.astype(F32)).astype(BF)
-    copied = jnp.broadcast_to(part[None], (GROUP, *part.shape))
+    copied = run_spread(part, other)
     full = all_pieces(copied, PLANES)
 
     split = (3 * D + 2 * H) // PIECE

time: 112 us -> 111 us (level)
  no operation moved by 1% of the time
where the time goes in v3:
time: 111 us
  blocking collectives  56.3 us (51%)
  starting transfers between devices  31 us (28%)
  Pallas kernels  15.7 us (14%)
  waiting for transfers between devices  7.11 us (6%)
    all_to_all x2, blocking collectives, all_pieces(): lax.all_to_all(value, ALL, 0, 0, axis_index_groups=groups, tiled=True)  56.3 us
    ppermute x1, starting transfers between devices, step(): from_next = lax.ppermute(list0, 'space', backward)  8.77 us
    pallas_call x1, Pallas kernels, run_layer(): pl.pallas_call(layer_kernel, out_shape=(jax.ShapeDtypeStruct((GROUP, PIEC...  7.62 us
    ppermute x1, starting transfers between devices, step(): from_next = lax.ppermute(back_prev, 'space', backward)  7.19 us
    ppermute x1, starting transfers between devices, step(): other = lax.ppermute(mine, 'hidden', swap)  5.37 us
    ppermute x1, starting transfers between devices, step(): other = lax.ppermute(part, ALL, across_z(False))  4.89 us
    ppermute x1, waiting for transfers between devices, step(): other = lax.ppermute(part, ALL, across_z(True))  3.76 us
    ppermute x1, starting transfers between devices, step(): first_other = lax.ppermute(edge_first, 'hidden', swap)  3.29 us
  transfers between devices with their start and end apart: 10, of which 3 were waited for; matrix products, arithmetic and copies ran while one was open for 0% of the time, Pallas kernels for 6%

profile of v3, /device:TPU:1, one launch (start us, length us, event | category | flops | bytes accessed | tf_op | source)
XLA Modules:
  0.0 111.1 jit_solution(3459089795838928845)
XLA Ops:
  0.6 3.3 %collective-permute-start.2 = (bf16[1536,256]{1,0:T(8,128)(2,1)}, bf16[1536,256]{1,0:T(8,128)(2,1)S(1)}, u32[]{:S(2)}, u32[]{:S(2)}) collective-permute-start(bf16[1536,256]{1,0:T(8,128)(2,1)} %refs_3_.1), channel_id=1, source_target_pairs={{0,1},{1,0},{2,3},{3,2},{4,5},{5,4},{6,7},{7,6},{8,9},{9,8},{10,11... | collective-permute-start | bytes 2359304 | tf_op jit(solution)/shard_map/ppermute | solution.py:598
  3.9 0.1 collective-permute-start.4
  4.0 0.4 collective-permute-start.3
  4.4 1.2 %pick.1 = (bf16[64,512]{1,0:T(8,128)(2,1)S(1)}, bf16[64,512]{1,0:T(8,128)(2,1)S(1)}) custom-call(s32[2,64]{1,0:T(2,128)} %bitcast.17, bf16[128,512]{1,0:T(8,128)(2,1)} %bitcast.21), custom_call_target="tpu_custom_call" | custom-call | flops 200000000 | bytes 400000 | tf_op jit(solution)/shard_map/pick/pallas_call | solution.py:105
  5.6 0.1 collective-permute-start
  5.7 8.8 %collective-permute-start.1 = (bf16[64,512]{1,0:T(8,128)(2,1)S(1)}, bf16[64,512]{1,0:T(8,128)(2,1)S(1)}, u32[]{:S(2)}, u32[]{:S(2)}) collective-permute-start(bf16[64,512]{1,0:T(8,128)(2,1)S(1)} %get-tuple-element.57), channel_id=1, source_target_pairs={{2,0},{4,2},{6,4},{8,6},{10,8},{12,10},{14,12},{16,14},{18,16},{20... | collective-permute-start | bytes 196616 | tf_op jit(solution)/shard_map/ppermute | solution.py:603
  14.5 2.6 %early.1 = (bf16[128,512]{1,0:T(8,128)(2,1)S(1)}, bf16[1536,256]{1,0:T(8,128)(2,1)S(1)}, f32[1,256]{1,0:T(1,128)S(1)}, bf16[1024,512]{1,0:T(8,128)(2,1)S(1)}, bf...) custom-call(s32[1,1024]{1,0:T(1,128)} %bitcast.25, ...), custom_call_target="tpu_custom_call" | custom-call | flops 1500000000 | bytes 8000000 | tf_op jit(solution)/shard_map/early/pallas_call | solution.py:155
  17.1 0.0 collective-permute-done.3.refs_17_
  17.1 0.0 collective-permute-done.refs_14_
  17.1 0.0 collective-permute-done.1.refs_15_
  17.1 0.0 collective-permute-done.4.refs_18_
  17.1 0.0 collective-permute-done.2.refs_16_
  17.2 7.6 %layer.1 = (bf16[32,232,128]{2,1,0:T(8,128)(2,1)S(1)}, bf16[1024,256]{1,0:T(8,128)(2,1)}, f32[128,256]{1,0:T(8,128)S(1)}, bf16[64,256]{1,0:T(8,128)(2,1)S(1)}, bf16[64,256]{1,0:T(8,128)(2,1)S(1)}) custom-call(bf16[128,512]{1,0:T(8,128)(2,1)S(1)} %get-tuple-element.42.refs_0_, bf16[1536,256]{1,0:T(8,128)(2,1)S(1)} %get-tuple-element.43.refs_1_, ...), custom_call_target="tpu_custom_call" | custom-call | flops 6000000000 | bytes 12000000 | tf_op jit(solution)/shard_map/layer/pallas_call | solution.py:325
  24.8 29.4 %all_to_all.10.pieces = bf16[32,232,128]{2,1,0:T(8,128)(2,1)S(1)} all-to-all(bf16[32,232,128]{2,1,0:T(8,128)(2,1)S(1)} %get-tuple-element.58), channel_id=1, replica_groups={{0,2,128,130,16,18,144,146,32,34,160,162,48,50,176,178,64,66,192,194,80..., dimensions={0} | all-to-all | bytes 3801088 | tf_op jit(solution)/shard_map/all_to_all | solution.py:567
  54.2 0.3 sum_pieces.1
  54.6 0.9 collective-permute-start.5
  55.5 3.8 %collective-permute-done.5 = bf16[232,128]{1,0:T(8,128)(2,1)S(1)} collective-permute-done((bf16[232,128]{1,0:T(8,128)(2,1)S(1)}, bf16[232,128]{1,0:T(8,128)(2,1)S(1)}, u32[]{:S(2)}, u32[]{:S(2)}) %collective-permute-start.5) | collective-permute-done | bytes 59424 | tf_op jit(solution)/shard_map/ppermute | solution.py:632
  59.3 4.9 %collective-permute-start.6 = (bf16[232,128]{1,0:T(8,128)(2,1)S(1)}, bf16[232,128]{1,0:T(8,128)(2,1)S(1)}, u32[]{:S(2)}, u32[]{:S(2)}) collective-permute-start(bf16[232,128]{1,0:T(8,128)(2,1)S(1)} %add_convert_fusion.part), channel_id=1, source_target_pairs={{0,12},{1,13},{2,14},{3,15},{4,8},{5,9},{6,10},{7,11},{8,4},{9,5},... | collective-permute-start | bytes 178184 | tf_op jit(solution)/shard_map/ppermute | solution.py:634
  64.2 2.0 %collective-permute-done.6.other = bf16[232,128]{1,0:T(8,128)(2,1)S(1)} collective-permute-done((bf16[232,128]{1,0:T(8,128)(2,1)S(1)}, bf16[232,128]{1,0:T(8,128)(2,1)S(1)}, u32[]{:S(2)}, u32[]{:S(2)}) %collective-permute-start.6) | collective-permute-done | bytes 59424 | tf_op jit(solution)/shard_map/ppermute | solution.py:634
  66.2 0.1 spread.1
  66.3 26.8 %all_to_all.11.full = bf16[32,232,128]{2,1,0:T(8,128)(2,1)S(1)} all-to-all(bf16[32,232,128]{2,1,0:T(8,128)(2,1)S(1)} %spread.1), channel_id=1, replica_groups={{0,2,128,130,16,18,144,146,32,34,160,162,48,50,176,178,64,66,192,194,80..., dimensions={0} | all-to-all | bytes 3801088 | tf_op jit(solution)/shard_map/all_to_all | solution.py:567
  93.1 0.1 slice.4
  93.2 5.4 %collective-permute-start.9 = (bf16[14,232,128]{2,1,0:T(8,128)(2,1)S(1)}, bf16[14,232,128]{2,1,0:T(8,128)(2,1)S(1)}, u32[]{:S(2)}, u32[]{:S(2)}) collective-permute-start(bf16[14,232,128]{2,1,0:T(8,128)(2,1)S(1)} %slice.4), channel_id=1, source_target_pairs={{0,1},{1,0},{2,3},{3,2},{4,5},{5,4},{6,7},{7,6},{8,9},{9,8},{10,11... | collective-permute-start | bytes 2494472 | tf_op jit(solution)/shard_map/ppermute | solution.py:640
  98.6 0.0 collective-permute-start.7
  98.6 7.2 %collective-permute-start.8 = (bf16[64,256]{1,0:T(8,128)(2,1)S(1)}, bf16[64,256]{1,0:T(8,128)(2,1)S(1)}, u32[]{:S(2)}, u32[]{:S(2)}) collective-permute-start(bf16[64,256]{1,0:T(8,128)(2,1)S(1)} %get-tuple-element.61), channel_id=1, source_target_pairs={{2,0},{4,2},{6,4},{8,6},{10,8},{12,10},{14,12},{16,14},{18,16},{20... | collective-permute-start | bytes 98312 | tf_op jit(solution)/shard_map/ppermute | solution.py:628
  105.7 1.3 %collective-permute-done.7.back_p = bf16[64,256]{1,0:T(8,128)(2,1)S(1)} collective-permute-done((bf16[64,256]{1,0:T(8,128)(2,1)S(1)}, bf16[64,256]{1,0:T(8,128)(2,1)S(1)}, u32[]{:S(2)}, u32[]{:S(2)}) %collective-permute-start.7) | collective-permute-done | bytes 32800 | tf_op jit(solution)/shard_map/ppermute | solution.py:629
  107.0 0.0 collective-permute-done.8.back_n
  107.0 2.6 %edge_out.1 = (f32[1536,256]{1,0:T(8,128)}, f32[256,512]{1,0:T(8,128)}, f32[1,256]{1,0:T(1,128)}, f32[1,512]{1,0:T(1,128)}, f32[1,512]{1,0:T(1,128)}, /*index=5*...) custom-call(bf16[32,232,128]{2,1,0:T(8,128)(2,1)S(1)} %all_to_all.11.full, ...), custom_call_target="tpu_custom_call" | custom-call | flops 1000000 | bytes 5000000 | tf_op jit(solution)/shard_map/edge_out/pallas_call | solution.py:464
  109.7 0.0 collective-permute-done.9.other
  109.7 1.2 %node_out.1 = (f32[1024,512]{1,0:T(8,128)}, f32[512,512]{1,0:T(8,128)}) custom-call(bf16[14,232,128]{2,1,0:T(8,128)(2,1)S(1)} %collective-permute-done.9.other, f32[1024,512]{1,0:T(8,128)} %get-tuple-element.68.first_in, f32[512,512]{1,0:T(8,128)} %get-tuple-element.69.second_in), custom_call_target="tpu_custom_call", output_to_operand_aliasing={{0}: (1, {}), {1}: (2, {})} | custom-call | flops 1000000 | bytes 2000000 | tf_op jit(solution)/shard_map/node_out/pallas_call | solution.py:504
  (1 shorter events, 0.0 us)
Async XLA Ops:
  0.6 16.5 %collective-permute-start.2 = (bf16[1536,256]{1,0:T(8,128)(2,1)}, bf16[1536,256]{1,0:T(8,128)(2,1)S(1)}, u32[]{:S(2)}, u32[]{:S(2)}) collective-permute-start(bf16[1536,256]{1,0:T(8,128)(2,1)} %refs_3_.1), channel_id=1, source_target_pairs={{0,1},{1,0},{2,3},{3,2},{4,5},{5,4},{6,7},{7,6},{8,9},{9,8},{10,11... | collective-permute-start | bytes 2359304 | tf_op jit(solution)/shard_map/ppermute | solution.py:598
  3.9 13.2 %collective-permute-start.4 = (bf16[256,512]{1,0:T(8,128)(2,1)}, bf16[256,512]{1,0:T(8,128)(2,1)S(1)}, u32[]{:S(2)}, u32[]{:S(2)}) collective-permute-start(bf16[256,512]{1,0:T(8,128)(2,1)} %refs_6_.1), channel_id=1, source_target_pairs={{0,1},{1,0},{2,3},{3,2},{4,5},{5,4},{6,7},{7,6},{8,9},{9,8},{10,11... | collective-permute-start | bytes 786440 | tf_op jit(solution)/shard_map/ppermute | solution.py:599
  4.0 13.1 %collective-permute-start.3 = (f32[1,256]{1,0:T(1,128)}, f32[1,256]{1,0:T(1,128)S(1)}, u32[]{:S(2)}, u32[]{:S(2)}) collective-permute-start(f32[1,256]{1,0:T(1,128)} %bitcast.33), channel_id=1, source_target_pairs={{0,1},{1,0},{2,3},{3,2},{4,5},{5,4},{6,7},{7,6},{8,9},{9,8},{10,11... | collective-permute-start | bytes 3080 | tf_op jit(solution)/shard_map/ppermute | solution.py:600
  5.6 11.5 %collective-permute-start = (bf16[64,512]{1,0:T(8,128)(2,1)S(1)}, bf16[64,512]{1,0:T(8,128)(2,1)S(1)}, u32[]{:S(2)}, u32[]{:S(2)}) collective-permute-start(bf16[64,512]{1,0:T(8,128)(2,1)S(1)} %get-tuple-element.56), channel_id=1, source_target_pairs={{0,2},{2,4},{4,6},{6,8},{8,10},{10,12},{12,14},{14,16},{16,18},{18... | collective-permute-start | bytes 196616 | tf_op jit(solution)/shard_map/ppermute | solution.py:602
  5.7 11.4 %collective-permute-start.1 = (bf16[64,512]{1,0:T(8,128)(2,1)S(1)}, bf16[64,512]{1,0:T(8,128)(2,1)S(1)}, u32[]{:S(2)}, u32[]{:S(2)}) collective-permute-start(bf16[64,512]{1,0:T(8,128)(2,1)S(1)} %get-tuple-element.57), channel_id=1, source_target_pairs={{2,0},{4,2},{6,4},{8,6},{10,8},{12,10},{14,12},{16,14},{18,16},{20... | collective-permute-start | bytes 196616 | tf_op jit(solution)/shard_map/ppermute | solution.py:603
  54.6 4.7 %collective-permute-start.5 = (bf16[232,128]{1,0:T(8,128)(2,1)S(1)}, bf16[232,128]{1,0:T(8,128)(2,1)S(1)}, u32[]{:S(2)}, u32[]{:S(2)}) collective-permute-start(bf16[232,128]{1,0:T(8,128)(2,1)S(1)} %sum_pieces.1), channel_id=1, source_target_pairs={{0,4},{1,5},{2,6},{3,7},{4,0},{5,1},{6,2},{7,3},{8,12},{9,13},{10,... | collective-permute-start | bytes 178184 | tf_op jit(solution)/shard_map/ppermute | solution.py:632
  59.3 6.9 %collective-permute-start.6 = (bf16[232,128]{1,0:T(8,128)(2,1)S(1)}, bf16[232,128]{1,0:T(8,128)(2,1)S(1)}, u32[]{:S(2)}, u32[]{:S(2)}) collective-permute-start(bf16[232,128]{1,0:T(8,128)(2,1)S(1)} %add_convert_fusion.part), channel_id=1, source_target_pairs={{0,12},{1,13},{2,14},{3,15},{4,8},{5,9},{6,10},{7,11},{8,4},{9,5},... | collective-permute-start | bytes 178184 | tf_op jit(solution)/shard_map/ppermute | solution.py:634
  93.2 16.5 %collective-permute-start.9 = (bf16[14,232,128]{2,1,0:T(8,128)(2,1)S(1)}, bf16[14,232,128]{2,1,0:T(8,128)(2,1)S(1)}, u32[]{:S(2)}, u32[]{:S(2)}) collective-permute-start(bf16[14,232,128]{2,1,0:T(8,128)(2,1)S(1)} %slice.4), channel_id=1, source_target_pairs={{0,1},{1,0},{2,3},{3,2},{4,5},{5,4},{6,7},{7,6},{8,9},{9,8},{10,11... | collective-permute-start | bytes 2494472 | tf_op jit(solution)/shard_map/ppermute | solution.py:640
  98.6 8.5 %collective-permute-start.7 = (bf16[64,256]{1,0:T(8,128)(2,1)S(1)}, bf16[64,256]{1,0:T(8,128)(2,1)S(1)}, u32[]{:S(2)}, u32[]{:S(2)}) collective-permute-start(bf16[64,256]{1,0:T(8,128)(2,1)S(1)} %get-tuple-element.60), channel_id=1, source_target_pairs={{0,2},{2,4},{4,6},{6,8},{8,10},{10,12},{12,14},{14,16},{16,18},{18... | collective-permute-start | bytes 98312 | tf_op jit(solution)/shard_map/ppermute | solution.py:629
  98.6 8.5 %collective-permute-start.8 = (bf16[64,256]{1,0:T(8,128)(2,1)S(1)}, bf16[64,256]{1,0:T(8,128)(2,1)S(1)}, u32[]{:S(2)}, u32[]{:S(2)}) collective-permute-start(bf16[64,256]{1,0:T(8,128)(2,1)S(1)} %get-tuple-element.61), channel_id=1, source_target_pairs={{2,0},{4,2},{6,4},{8,6},{10,8},{12,10},{14,12},{16,14},{18,16},{20... | collective-permute-start | bytes 98312 | tf_op jit(solution)/shard_map/ppermute | solution.py:628
